TPU v7x, 256 devices: a whole 4x4x8 slice. The times are simulated.
256 devices in a mesh: group: 16 (over z_hi, x), shard: 16 (over z_lo, y, core).
Axes of the slice: x: 4, y: 4, z: 8 (z_hi: 4, z_lo: 2; z = z_hi * 2 + z_lo), core: 2. Of those that a mesh axis runs over, the one named last changes fastest.
Arguments:
- entity: float32 [131072, 400], P(('group', 'shard')), may hold values from -6 to 6
- entity_state: float32 [131072], P(('group', 'shard')), may hold values from 0.1 to 10
- relation: float32 [1345, 400], replicated, may hold values from -6 to 6
- relation_state: float32 [1345], replicated, may hold values from 10 to 1000
- src_send: int32 [256, 16, 64], P(('group', 'shard')), may hold values from 0 to 511
- dst_send: int32 [256, 16, 64], P(('group', 'shard')), may hold values from 0 to 511
- edge_source: int32 [262144], P(('group', 'shard')), may hold values from 0 to 1023
- edge_relation: int32 [262144], P(('group', 'shard')), may hold values from 0 to 1344
- edge_target: int32 [262144], P(('group', 'shard')), may hold values from 0 to 1023
- neg_slots: int32 [512, 1000], P(('group', 'shard')), may hold values from 0 to 1023
- edge_count: int32 [256], P(('group', 'shard')), may hold values from 1 to 1024, 87381 in all
Outputs:
- entity_new: float32 [131072, 400], P(('group', 'shard'))
- relation_new: float32 [1345, 400], replicated
- edge_loss: float32 [262144], P(('group', 'shard'))
Inputs may be any that keep to these rules, and one draw needn't show every extreme that they name: The live edges of a device are its first edge_count slots; some device has all 1024 live.
All inputs are finite; a program needn't handle non-finite values.
Results may differ from a plain program's by a relative error of at most 0.0003.
Values sent between devices are 32-bit elements; how exact they have to be, the bound alone decides.
A program may use at most 128 MiB of HBM per device.

v0:
```python
import jax
import jax.numpy as jnp
from jax import lax
from jax.sharding import PartitionSpec as P

SPAN = 512


learn_rate = 0.5


def passed_along(value, axis, by):
    count = lax.axis_size(axis)
    return lax.ppermute(value, axis, [(i, (i + by) % count) for i in range(count)])


def complex_product(multiplier, multiplicand):
    half_width = multiplier.shape[1] // 2
    first_real, first_imag = (multiplier[:, :half_width], multiplier[:, half_width:])
    second_real, second_imag = (multiplicand[:, :half_width], multiplicand[:, half_width:])
    return jnp.concatenate(
        [
            first_real * second_real - first_imag * second_imag,
            first_real * second_imag + first_imag * second_real,
        ],
        axis=1,
    )


def conj_product(multiplier, multiplicand):
    half_width = multiplier.shape[1] // 2
    first_real, first_imag = (multiplier[:, :half_width], multiplier[:, half_width:])
    second_real, second_imag = (multiplicand[:, :half_width], multiplicand[:, half_width:])
    return jnp.concatenate(
        [
            first_real * second_real + first_imag * second_imag,
            first_imag * second_real - first_real * second_imag,
        ],
        axis=1,
    )


def span_terms(queries, tail_rows, negatives, live_mask):
    pos_score = jnp.sum(queries * tail_rows, axis=1)
    neg_score = jnp.dot(queries, negatives.T, precision=lax.Precision.HIGHEST)
    score_peak = jnp.maximum(pos_score, jnp.max(neg_score, axis=1))
    exp_total = jnp.exp(pos_score - score_peak) + jnp.sum(
        jnp.exp(neg_score - score_peak[:, None]), axis=1
    )
    log_total = score_peak + jnp.log(exp_total)
    edge_loss = (log_total - pos_score) * live_mask
    pos_grad = (jnp.exp(pos_score - log_total) - 1.0) * live_mask
    neg_grad = jnp.exp(neg_score - log_total[:, None]) * live_mask[:, None]
    neg_query = jnp.dot(neg_grad, negatives, precision=lax.Precision.HIGHEST)
    negative_grad = lax.dot_general(
        neg_grad, queries, (((0,), (0,)), ((), ())), precision=lax.Precision.HIGHEST
    )
    return (edge_loss, pos_grad, neg_query, negative_grad)


def adagrad(params, accumulator, gradient):
    new_state = accumulator + jnp.mean(gradient * gradient, axis=1)
    return params - learn_rate * gradient / jnp.sqrt(new_state)[:, None]


def on_device(
    entity,
    entity_state,
    relation,
    relation_state,
    src_send,
    dst_send,
    edge_source,
    edge_relation,
    edge_target,
    neg_slots,
    edge_count,
):
    feature_count = entity.shape[1]
    peer_count, block_size = (src_send.shape[1], src_send.shape[2])
    table_rows = peer_count * block_size
    edge_rows = edge_source.shape[0]
    spans = edge_rows // SPAN
    sent_source = lax.all_to_all(
        entity[src_send[0]], "shard", split_axis=0, concat_axis=0, tiled=True
    )
    source_table = sent_source.reshape(table_rows, feature_count)
    moved_entity, moved_index = passed_along((entity, dst_send), "group", -1)
    target_blocks = lax.all_to_all(
        moved_entity[moved_index[0]], "shard", split_axis=0, concat_axis=0, tiled=True
    )
    target_table = target_blocks.reshape(table_rows, feature_count)
    live_count = edge_count[0]
    live_mask = (jnp.arange(edge_rows, dtype=jnp.int32) < live_count).astype(jnp.float32)
    head_rows = source_table[edge_source]
    tail_rows = target_table[edge_target]
    rel_rows = relation[edge_relation]
    queries = complex_product(head_rows, rel_rows)

    def span_turn(position, carried):
        loss_all, pos_all, query_all, target_grad = carried
        first_row = position * SPAN
        slots = neg_slots[position]
        edge_loss, pos_grad, neg_query, negative_grad = span_terms(
            lax.dynamic_slice_in_dim(queries, first_row, SPAN),
            lax.dynamic_slice_in_dim(tail_rows, first_row, SPAN),
            target_table[slots],
            lax.dynamic_slice_in_dim(live_mask, first_row, SPAN),
        )
        loss_all = lax.dynamic_update_slice_in_dim(loss_all, edge_loss, first_row, 0)
        pos_all = lax.dynamic_update_slice_in_dim(pos_all, pos_grad, first_row, 0)
        query_all = lax.dynamic_update_slice_in_dim(query_all, neg_query, first_row, 0)
        target_grad = target_grad.at[slots].add(negative_grad)
        return (loss_all, pos_all, query_all, target_grad)

    initial = (
        jnp.zeros((edge_rows,), jnp.float32),
        jnp.zeros((edge_rows,), jnp.float32),
        jnp.zeros((edge_rows, feature_count), jnp.float32),
        jnp.zeros((table_rows, feature_count), jnp.float32),
    )
    edge_loss, pos_grad, neg_query, target_grad = lax.fori_loop(0, spans, span_turn, initial)
    query_grad = pos_grad[:, None] * tail_rows + neg_query
    target_grad = target_grad.at[edge_target].add(pos_grad[:, None] * queries)
    source_grad = (
        jnp.zeros((table_rows, feature_count), jnp.float32)
        .at[edge_source]
        .add(conj_product(query_grad, rel_rows))
    )
    relation_part = (
        jnp.zeros(relation.shape, jnp.float32)
        .at[edge_relation]
        .add(conj_product(query_grad, head_rows))
    )
    relation_total = lax.psum(relation_part, ("group", "shard"))
    returned_source = lax.all_to_all(
        source_grad.reshape(peer_count, block_size, feature_count),
        "shard",
        split_axis=0,
        concat_axis=0,
        tiled=True,
    )
    entity_grad = (
        jnp.zeros(entity.shape, jnp.float32)
        .at[src_send[0].reshape(-1)]
        .add(returned_source.reshape(-1, feature_count))
    )
    target_blocks_grad = target_grad.reshape(peer_count, block_size, feature_count)
    returned_blocks = lax.all_to_all(
        target_blocks_grad, "shard", split_axis=0, concat_axis=0, tiled=True
    )
    dense_grad = (
        jnp.zeros(entity.shape, jnp.float32)
        .at[moved_index[0].reshape(-1)]
        .add(returned_blocks.reshape(-1, feature_count))
    )
    entity_grad = entity_grad + passed_along(dense_grad, "group", 1)
    return (
        adagrad(entity, entity_state, entity_grad),
        adagrad(relation, relation_state, relation_total),
        edge_loss,
    )


def solution(mesh):
    return jax.shard_map(
        on_device,
        mesh=mesh,
        in_specs=(
            P(("group", "shard"), None),
            P(("group", "shard")),
            P(),
            P(),
            P(("group", "shard"), None, None),
            P(("group", "shard"), None, None),
            P(("group", "shard")),
            P(("group", "shard")),
            P(("group", "shard")),
            P(("group", "shard"), None),
            P(("group", "shard")),
        ),
        out_specs=(P(("group", "shard"), None), P(), P(("group", "shard"))),
        check_vma=False,
    )
```

profile of v0, /device:TPU:8, one launch (start us, length us, event | category | flops | bytes accessed | tf_op | source)
XLA Modules:
  0.0 595.1 jit_solution(1953775435204047000)
XLA Ops:
  14.3 6.5 %all-to-all-start = ((f32[16,64,400]{2,1,0:T(8,128)}), f32[16,64,400]{2,1,0:T(8,128)}, u32[]{:S(2)}, u32[]{:S(2)}) async-start(f32[16,64,400]{2,1,0:T(8,128)} %bitcast.37), calls=%async_computation | async-start | bytes 4194304 | tf_op jit(solution)/shard_map/all_to_all | solution.py:84
  20.8 7.6 %collective-permute-start.1 = (f32[512,400]{0,1:T(8,128)S(1)}, f32[512,400]{0,1:T(8,128)S(1)}, u32[]{:S(2)}, u32[]{:S(2)}) collective-permute-start(f32[512,400]{0,1:T(8,128)S(1)} %copy-done.11), channel_id=1, source_target_pairs={{0,240},{16,0},{32,16},{48,32},{64,48},{80,64},{96,80},{112,96},{1... | collective-permute-start | bytes 2457608 | tf_op jit(solution)/shard_map/ppermute | solution.py:14
  29.3 17.2 %collective-permute-done = s32[1,16,64]{2,1,0:T(8,128)S(1)} collective-permute-done((s32[1,16,64]{2,1,0:T(8,128)S(1)}, s32[1,16,64]{2,1,0:T(8,128)S(1)}, u32[]{:S(2)}, u32[]{:S(2)}) %collective-permute-start) | collective-permute-done | bytes 4128 | tf_op jit(solution)/shard_map/ppermute | solution.py:14
  51.8 7.4 %all-to-all-done = f32[16,64,400]{2,1,0:T(8,128)} async-done(((f32[16,64,400]{2,1,0:T(8,128)}), f32[16,64,400]{2,1,0:T(8,128)}, u32[]{:S(2)}, u32[]{:S(2)}) %all-to-all-start) | async-done | bytes 1638432 | tf_op jit(solution)/shard_map/all_to_all | solution.py:84
  59.3 32.5 %all-to-all-start.1 = ((f32[16,64,400]{2,1,0:T(8,128)}), f32[16,64,400]{2,1,0:T(8,128)S(1)}, u32[]{:S(2)}, u32[]{:S(2)}) async-start(f32[16,64,400]{2,1,0:T(8,128)} %bitcast.36), calls=%async_computation.1 | async-start | bytes 4194304 | tf_op jit(solution)/shard_map/all_to_all | solution.py:89
  95.8 7.1 %gather_fusion.3 = f32[1024,400]{1,0:T(8,128)} fusion(f32[1345,400]{1,0:T(8,128)} %copy.32, s32[1024]{0:T(1024)S(1)} %get-tuple-element.322), kind=kCustom, calls=%fused_computation.3 | custom fusion | bytes 3280896 | tf_op jit(solution)/shard_map/gather | solution.py:97
  102.9 6.9 %gather_fusion.2 = f32[1024,400]{1,0:T(8,128)} fusion(f32[1024,400]{1,0:T(8,128)} %bitcast.5, s32[1024]{0:T(1024)S(1)} %get-tuple-element.324), kind=kCustom, calls=%fused_computation.2 | custom fusion | bytes 3280896 | tf_op jit(solution)/shard_map/gather | solution.py:95
  126.8 68.5 %while.21 = (s32[]{:T(128)}, f32[1024]{0:T(1024)S(1)}, f32[1024]{0:T(1024)S(1)}, f32[1024,400]{0,1:T(8,128)}, f32[1024,400]{1,0:T(8,128)}, /*index=5*/f32[1024,4...) while((s32[]{:T(128)}, f32[1024]{0:T(1024)S(1)}, ...), condition=%wide.region_5.0_spmd, body=%wide.region_0.0_spmd.sunk | while | flops 7377200640 | bytes 52573032 | solution.py:122
  133.6 5.4 fusion.40
  146.0 4.9 fusion.42
  151.0 10.1 %scatter_fusion = f32[1024,400]{1,0:T(8,128)} fusion(f32[1024,400]{1,0:T(8,128)} %get-tuple-element.416, s32[1000]{0:T(1024)S(1)} %bitcast.39, f32[1000,400]{1,0:T(8,128)} %fusion.42), kind=kCustom, calls=%fused_computation.6.clone.1 | custom fusion | flops 400000 | bytes 4804000 | tf_op jit(solution)/shard_map/while/body/eval_jaxpr/scatter-add | solution.py:113
  167.7 5.4 fusion.40
  180.1 4.9 fusion.42
  185.1 10.1 %scatter_fusion = f32[1024,400]{1,0:T(8,128)} fusion(f32[1024,400]{1,0:T(8,128)} %get-tuple-element.416, s32[1000]{0:T(1024)S(1)} %bitcast.39, f32[1000,400]{1,0:T(8,128)} %fusion.42), kind=kCustom, calls=%fused_computation.6.clone.1 | custom fusion | flops 400000 | bytes 4804000 | tf_op jit(solution)/shard_map/while/body/eval_jaxpr/scatter-add | solution.py:113
  195.4 10.6 %scatter_custom_fusion.1 = f32[1024,400]{1,0:T(8,128)} fusion(f32[1024,400]{1,0:T(8,128)} %get-tuple-element.248, s32[1024]{0:T(1024)S(1)} %get-tuple-element.325, f32[1024]{0:T(1024)S(1)} %get-tuple-element.249, f32[1024,200]{1,0:T(8,128)} %copy-done.7, f32[1024,200]{1,0:T(8,128)S(1)} %get-tuple-element.317), kind=kCustom, calls=%fused_computation.44 | custom fusion | flops 1228800 | bytes 3739648 | tf_op jit(solution)/shard_map/scatter-add | solution.py:124
  205.9 6.7 %all-to-all-start.2 = ((f32[16,64,400]{2,1,0:T(8,128)}), f32[16,64,400]{2,1,0:T(8,128)}, u32[]{:S(2)}, u32[]{:S(2)}) async-start(f32[16,64,400]{2,1,0:T(8,128)} %bitcast.35), calls=%async_computation.2 | async-start | bytes 4194304 | tf_op jit(solution)/shard_map/all_to_all | solution.py:149
  220.4 8.5 %scatter_custom_fusion.3 = f32[1024,400]{1,0:T(8,128)} fusion(s32[1024]{0:T(1024)S(1)} %get-tuple-element.323, f32[1024,200]{1,0:T(8,128)S(1)} %get-tuple-element.319, f32[]{:T(128)} %constant.108, f32[1024,200]{1,0:T(8,128)S(1)} %get-tuple-element.320, f32[]{:T(128)} %constant.97.clone.1), kind=kCustom, calls=%fused_computation.35 | custom fusion | flops 819200 | bytes 3735560 | tf_op jit(solution)/shard_map/scatter-add | solution.py:128
  228.9 10.9 %all-to-all-done.2 = f32[16,64,400]{2,1,0:T(8,128)} async-done(((f32[16,64,400]{2,1,0:T(8,128)}), f32[16,64,400]{2,1,0:T(8,128)}, u32[]{:S(2)}, u32[]{:S(2)}) %all-to-all-start.2) | async-done | bytes 1638432 | tf_op jit(solution)/shard_map/all_to_all | solution.py:149
  239.8 6.9 %all-to-all-start.3 = ((f32[16,64,400]{2,1,0:T(8,128)}), f32[16,64,400]{2,1,0:T(8,128)}, u32[]{:S(2)}, u32[]{:S(2)}) async-start(f32[16,64,400]{2,1,0:T(8,128)} %bitcast.13), calls=%async_computation.3 | async-start | bytes 4194304 | tf_op jit(solution)/shard_map/all_to_all | solution.py:136
  246.8 9.0 %scatter_custom_fusion.5 = f32[1345,400]{1,0:T(8,128)} fusion(s32[1024]{0:T(1024)S(1)} %get-tuple-element.321, f32[1024,200]{1,0:T(8,128)S(1)} %copy-done.10, f32[]{:T(128)} %constant.108, f32[1024,200]{1,0:T(8,128)S(1)} %get-tuple-element.313, f32[]{:T(128)} %constant.97.clone.1), kind=kCustom, calls=%fused_computation.39 | custom fusion | flops 819200 | bytes 4249160 | tf_op jit(solution)/shard_map/scatter-add | solution.py:133
  256.7 271.1 %all-reduce.2.cloned.1.call-done = f32[1345,400]{1,0:T(8,128)} async-done(((f32[1345,400]{1,0:T(8,128)}), f32[1345,400]{1,0:T(8,128)}) %all-reduce.2.cloned.1.call-update) | async-done | bytes 2152016 | tf_op jit(solution)/shard_map/psum | solution.py:135
  529.9 7.5 %scatter_custom_fusion.2 = f32[512,400]{1,0:T(8,128)S(1)} fusion(s32[1024]{0:T(1024)S(1)} %bitcast.41, f32[1024,400]{1,0:T(8,128)} %bitcast.11, f32[]{:T(128)} %constant.97.clone.1), kind=kCustom, calls=%fused_computation.57 | custom fusion | flops 409600 | bytes 819712 | tf_op jit(solution)/shard_map/scatter-add | solution.py:155
  547.0 31.1 %collective-permute-done.2 = f32[512,400]{0,1:T(8,128)S(1)} collective-permute-done((f32[512,400]{0,1:T(8,128)S(1)}, f32[512,400]{0,1:T(8,128)S(1)}, u32[]{:S(2)}, u32[]{:S(2)}) %collective-permute-start.2) | collective-permute-done | bytes 819232 | tf_op jit(solution)/shard_map/ppermute | solution.py:14
  578.4 7.7 %scatter_fusion.1 = f32[512,400]{1,0:T(8,128)S(1)} fusion(f32[512,400]{1,0:T(8,128)S(1)} %copy.37, s32[1024]{0:T(1024)S(1)} %bitcast.40, f32[1024,400]{1,0:T(8,128)} %bitcast.14), kind=kCustom, calls=%fused_computation.10 | custom fusion | flops 409600 | bytes 4919296 | tf_op jit(solution)/shard_map/scatter-add | solution.py:146
  (114 shorter events, 82.9 us)
Async XLA Ops:
  8.6 5.7 copy-start.1
  14.3 6.5 %copy-start.11 = (f32[512,400]{0,1:T(8,128)S(1)}, f32[512,400]{0,1:T(8,128)}, u32[]{:S(2)}) copy-start(f32[512,400]{0,1:T(8,128)} %param.13) | copy-start | bytes 2457604
  14.3 14.1 %copy-start.20 = (s32[1,16,64]{2,1,0:T(8,128)S(1)}, s32[1,16,64]{2,1,0:T(8,128)}, u32[]{:S(2)}) copy-start(s32[1,16,64]{2,1,0:T(8,128)} %param.18) | copy-start | bytes 12292
  14.3 44.9 %all-to-all-start = ((f32[16,64,400]{2,1,0:T(8,128)}), f32[16,64,400]{2,1,0:T(8,128)}, u32[]{:S(2)}, u32[]{:S(2)}) async-start(f32[16,64,400]{2,1,0:T(8,128)} %bitcast.37), calls=%async_computation | async-start | bytes 4194304 | tf_op jit(solution)/shard_map/all_to_all | solution.py:84
  20.8 25.7 %collective-permute-start.1 = (f32[512,400]{0,1:T(8,128)S(1)}, f32[512,400]{0,1:T(8,128)S(1)}, u32[]{:S(2)}, u32[]{:S(2)}) collective-permute-start(f32[512,400]{0,1:T(8,128)S(1)} %copy-done.11), channel_id=1, source_target_pairs={{0,240},{16,0},{32,16},{48,32},{64,48},{80,64},{96,80},{112,96},{1... | collective-permute-start | bytes 2457608 | tf_op jit(solution)/shard_map/ppermute | solution.py:14
  28.4 18.0 %collective-permute-start = (s32[1,16,64]{2,1,0:T(8,128)S(1)}, s32[1,16,64]{2,1,0:T(8,128)S(1)}, u32[]{:S(2)}, u32[]{:S(2)}) collective-permute-start(s32[1,16,64]{2,1,0:T(8,128)S(1)} %copy-done.20), channel_id=1, source_target_pairs={{0,240},{16,0},{32,16},{48,32},{64,48},{80,64},{96,80},{112,96},{1... | collective-permute-start | bytes 12296 | tf_op jit(solution)/shard_map/ppermute | solution.py:14
  59.3 59.7 %all-to-all-start.1 = ((f32[16,64,400]{2,1,0:T(8,128)}), f32[16,64,400]{2,1,0:T(8,128)S(1)}, u32[]{:S(2)}, u32[]{:S(2)}) async-start(f32[16,64,400]{2,1,0:T(8,128)} %bitcast.36), calls=%async_computation.1 | async-start | bytes 4194304 | tf_op jit(solution)/shard_map/all_to_all | solution.py:89
  91.7 4.0 copy-start.15
  95.7 7.1 %copy-start.16 = (s32[1024]{0:T(1024)S(1)}, s32[1024]{0:T(1024)}, u32[]{:S(2)}) copy-start(s32[1024]{0:T(1024)} %param.19) | copy-start | bytes 12292
  95.7 7.1 %copy-start.17 = (s32[1024]{0:T(1024)S(1)}, s32[1024]{0:T(1024)}, u32[]{:S(2)}) copy-start(s32[1024]{0:T(1024)} %param.21) | copy-start | bytes 12292
  133.6 6.1 %copy-start.8 = (f32[1024,400]{0,1:T(8,128)S(1)}, f32[1024,400]{0,1:T(8,128)}, u32[]{:S(2)}) copy-start(f32[1024,400]{0,1:T(8,128)} %get-tuple-element.415) | copy-start | bytes 4915204 | tf_op jit(solution)/shard_map/while
  140.6 5.4 copy-start.3
  167.7 6.1 %copy-start.8 = (f32[1024,400]{0,1:T(8,128)S(1)}, f32[1024,400]{0,1:T(8,128)}, u32[]{:S(2)}) copy-start(f32[1024,400]{0,1:T(8,128)} %get-tuple-element.415) | copy-start | bytes 4915204 | tf_op jit(solution)/shard_map/while
  174.7 5.4 copy-start.3
  195.4 10.6 %copy-start.18 = (f32[1024]{0:T(1024)}, f32[1024]{0:T(1024)S(1)}, u32[]{:S(2)}) copy-start(f32[1024]{0:T(1024)S(1)} %get-tuple-element.287) | copy-start | bytes 12292
  205.9 33.9 %all-to-all-start.2 = ((f32[16,64,400]{2,1,0:T(8,128)}), f32[16,64,400]{2,1,0:T(8,128)}, u32[]{:S(2)}, u32[]{:S(2)}) async-start(f32[16,64,400]{2,1,0:T(8,128)} %bitcast.35), calls=%async_computation.2 | async-start | bytes 4194304 | tf_op jit(solution)/shard_map/all_to_all | solution.py:149
  212.6 3.1 copy-start.4
  239.8 6.9 %copy-start.10 = (f32[1024,200]{1,0:T(8,128)S(1)}, f32[1024,200]{1,0:T(8,128)}, u32[]{:S(2)}) copy-start(f32[1024,200]{1,0:T(8,128)} %get-tuple-element.314) | copy-start | bytes 2457604
  239.8 338.6 %all-to-all-start.3 = ((f32[16,64,400]{2,1,0:T(8,128)}), f32[16,64,400]{2,1,0:T(8,128)}, u32[]{:S(2)}, u32[]{:S(2)}) async-start(f32[16,64,400]{2,1,0:T(8,128)} %bitcast.13), calls=%async_computation.3 | async-start | bytes 4194304 | tf_op jit(solution)/shard_map/all_to_all | solution.py:136
  246.7 281.1 %all-reduce.2.cloned.1.call-start = ((), (), s32[]{:S(2)}) async-start(), calls=%async_computation.4 | async-start | bytes 5537792 | tf_op jit(solution)/shard_map/psum | solution.py:135
  529.9 9.2 %copy-start.14 = (f32[1345]{0:T(1024)S(1)}, f32[1345]{0:T(1024)}, u32[]{:S(2)}) copy-start(f32[1345]{0:T(1024)} %param.16) | copy-start | bytes 16144
  537.7 40.4 %collective-permute-start.2 = (f32[512,400]{0,1:T(8,128)S(1)}, f32[512,400]{0,1:T(8,128)S(1)}, u32[]{:S(2)}, u32[]{:S(2)}) collective-permute-start(f32[512,400]{0,1:T(8,128)S(1)} %copy.35), channel_id=1, source_target_pairs={{0,16},{16,32},{32,48},{48,64},{64,80},{80,96},{96,112},{112,128},... | collective-permute-start | bytes 2457608 | tf_op jit(solution)/shard_map/ppermute | solution.py:14
  578.4 7.9 %copy-start.19 = (f32[512]{0:T(512)S(1)}, f32[512]{0:T(512)}, u32[]{:S(2)}) copy-start(f32[512]{0:T(512)} %param.14) | copy-start | bytes 6148
  578.4 7.9 %copy-start.2 = (f32[512,400]{1,0:T(8,128)S(1)}, f32[512,400]{1,0:T(8,128)}, u32[]{:S(2)}) copy-start(f32[512,400]{1,0:T(8,128)} %copy-done.1) | copy-start | bytes 2457604
  (9 other events, 15.2 us)
Sparse Core Ops, SparseCore 0:
  256.0 271.8 all-reduce.1
where the time goes:
time: 601 us; the launch traced here: 595 us
  waiting for transfers between devices  341 us (57%)
  other arithmetic  85 us (14%)
  starting transfers between devices  62.4 us (10%)
  local copies, waits for them, and re-layouts  61.8 us (10%)
  matrix products  29.2 us (5%)
  between operations  15.4 us (3%)
    psum x1, waiting for transfers between devices, on_device(): relation_total = lax.psum(relation_part, ('group', 'shard'))  271 us
    ppermute x3, waiting for transfers between devices, passed_along(): lax.ppermute(value, axis, [(i, (i + by) % count) for i in range(count)])  48.2 us
    all_to_all x1, starting transfers between devices, on_device(): lax.all_to_all(moved_entity[moved_index[0]], 'shard', split_axis=0, conca...  32.5 us
    scatter-add x2, other arithmetic, span_turn(): target_grad = target_grad.at[slots].add(negative_grad)  20.2 us
  transfers between devices with their start and end apart: 8, of which 6 were waited for; matrix products, arithmetic and copies ran while one was open for 12% of the time, Pallas kernels for 0%

commit v1 on v0

v1 whole, which is shorter than its diff:
```python
import functools

import jax
import jax.numpy as jnp
from jax import lax
from jax.experimental import pallas as pl
from jax.experimental.pallas import tpu as pltpu
from jax.sharding import PartitionSpec as P

SPAN = 512
LEARN_RATE = 0.5
HALF = 256
WIDE = 2 * HALF

NT = (((1,), (1,)), ((), ()))
NN = (((1,), (0,)), ((), ()))
TN = (((0,), (0,)), ((), ()))


def split2(x):
    hi = x.astype(jnp.bfloat16)
    lo = (x - hi.astype(jnp.float32)).astype(jnp.bfloat16)
    return hi, lo


def split3(x):
    hi = x.astype(jnp.bfloat16)
    rest = x - hi.astype(jnp.float32)
    mid = rest.astype(jnp.bfloat16)
    lo = (rest - mid.astype(jnp.float32)).astype(jnp.bfloat16)
    return hi, mid, lo


def mxu(a, b, dims):
    return lax.dot_general(a, b, dims, preferred_element_type=jnp.float32)


def wide(x):
    half = x.shape[1] // 2
    pad = ((0, 0), (0, HALF - half))
    return jnp.concatenate([jnp.pad(x[:, :half], pad), jnp.pad(x[:, half:], pad)], axis=1)


def narrow(x, width):
    half = width // 2
    return jnp.concatenate([x[:, :half], x[:, HALF : HALF + half]], axis=1)


def product(a, b):
    ar, ai, br, bi = a[:, :HALF], a[:, HALF:], b[:, :HALF], b[:, HALF:]
    return jnp.concatenate([ar * br - ai * bi, ar * bi + ai * br], axis=1)


def conj_product(a, b):
    ar, ai, br, bi = a[:, :HALF], a[:, HALF:], b[:, :HALF], b[:, HALF:]
    return jnp.concatenate([ar * br + ai * bi, ai * br - ar * bi], axis=1)


def chosen(index, count):
    lanes = lax.broadcasted_iota(jnp.int32, (index.shape[0], count), 1)
    return jnp.where(lanes == index, 1.0, 0.0).astype(jnp.bfloat16)


def vmem(shape, index_map):
    return pl.BlockSpec(shape, index_map, memory_space=pltpu.VMEM)


def params(limit=48 << 20):
    return pltpu.CompilerParams(vmem_limit_bytes=limit)


def take_kernel(index_ref, table_ref, out_ref, parts_ref):
    @pl.when(pl.program_id(0) == 0)
    def _():
        for k, part in enumerate(split3(table_ref[...])):
            parts_ref[k] = part

    pick = chosen(index_ref[...], table_ref.shape[0])
    out_ref[...] = (
        mxu(pick, parts_ref[0], NN) + mxu(pick, parts_ref[1], NN)
    ) + mxu(pick, parts_ref[2], NN)


def take_rows(table, index):
    rows, count = index.shape[0], table.shape[0]
    tile = min(256, rows)
    return pl.pallas_call(
        take_kernel,
        grid=(rows // tile,),
        in_specs=[vmem((tile, 1), lambda i: (i, 0)), vmem((count, WIDE), lambda i: (0, 0))],
        out_specs=vmem((tile, WIDE), lambda i: (i, 0)),
        out_shape=jax.ShapeDtypeStruct((rows, WIDE), jnp.float32),
        scratch_shapes=[pltpu.VMEM((3, count, WIDE), jnp.bfloat16)],
        compiler_params=params(),
        cost_estimate=pl.CostEstimate(
            flops=6 * rows * count * WIDE, bytes_accessed=4 * (rows + count) * WIDE, transcendentals=0
        ),
        name="take_rows",
    )(index, table)


def query_kernel(index_ref, table_ref, rel_ref, head_ref, query_ref, parts_ref):
    @pl.when(pl.program_id(0) == 0)
    def _():
        for k, part in enumerate(split3(table_ref[...])):
            parts_ref[k] = part

    pick = chosen(index_ref[...], table_ref.shape[0])
    heads = (mxu(pick, parts_ref[0], NN) + mxu(pick, parts_ref[1], NN)) + mxu(pick, parts_ref[2], NN)
    head_ref[...] = heads
    query_ref[...] = product(heads, rel_ref[...])


def make_queries(table, index, rels):
    rows, count = index.shape[0], table.shape[0]
    tile = min(256, rows)
    block = vmem((tile, WIDE), lambda i: (i, 0))
    shape = jax.ShapeDtypeStruct((rows, WIDE), jnp.float32)
    return pl.pallas_call(
        query_kernel,
        grid=(rows // tile,),
        in_specs=[vmem((tile, 1), lambda i: (i, 0)), vmem((count, WIDE), lambda i: (0, 0)), block],
        out_specs=[block, block],
        out_shape=[shape, shape],
        scratch_shapes=[pltpu.VMEM((3, count, WIDE), jnp.bfloat16)],
        compiler_params=params(),
        cost_estimate=pl.CostEstimate(
            flops=6 * rows * count * WIDE, bytes_accessed=4 * (4 * rows + count) * WIDE, transcendentals=0
        ),
        name="make_queries",
    )(index, table, rels)


def span_kernel(
    count_ref, target_ref, slots_ref, query_ref, table_ref,
    loss_ref, query_grad_ref, target_grad_ref,
    score_ref, times_ref, parts_ref, query_parts_ref,
):
    span = pl.program_id(0)
    table_rows = table_ref.shape[0]
    tile = min(256, table_rows)
    tiles = table_rows // tile

    @pl.when(span == 0)
    def _():
        for k, part in enumerate(split3(table_ref[...])):
            parts_ref[k] = part

    for k, part in enumerate(split3(query_ref[...])):
        query_parts_ref[k] = part

    edge = lax.broadcasted_iota(jnp.int32, (1, SPAN), 1) + span * SPAN
    live = jnp.where(edge < count_ref[0], 1.0, 0.0)
    target = target_ref[0]
    slots = slots_ref[0]

    def score_turn(t, carried):
        peak, pos = carried
        rows = pl.ds(pl.multiple_of(t * tile, tile), tile)
        t0, t1, t2 = parts_ref[0, rows], parts_ref[1, rows], parts_ref[2, rows]
        q0, q1, q2 = query_parts_ref[0], query_parts_ref[1], query_parts_ref[2]
        small = mxu(t0, q2, NT) + mxu(t2, q0, NT) + mxu(t1, q1, NT)
        score = (small + (mxu(t0, q1, NT) + mxu(t1, q0, NT))) + mxu(t0, q0, NT)
        score_ref[rows] = score
        number = lax.broadcasted_iota(jnp.int32, (tile, 1), 0) + t * tile
        times = jnp.sum(jnp.where(slots == number, 1.0, 0.0), axis=1, keepdims=True)
        times_ref[rows] = times
        used = jnp.where(times > 0.0, score, -jnp.inf)
        peak = jnp.maximum(peak, jnp.max(used, axis=0, keepdims=True))
        pos = pos + jnp.sum(jnp.where(target == number, score, 0.0), axis=0, keepdims=True)
        return peak, pos

    start = (jnp.full((1, SPAN), -jnp.inf, jnp.float32), jnp.zeros((1, SPAN), jnp.float32))
    peak, pos = lax.fori_loop(0, tiles, score_turn, start)
    peak = jnp.maximum(peak, pos)

    def total_turn(t, total):
        rows = pl.ds(pl.multiple_of(t * tile, tile), tile)
        times = times_ref[rows]
        value = jnp.where(times > 0.0, times * jnp.exp(score_ref[rows] - peak), 0.0)
        score_ref[rows] = value
        return total + jnp.sum(value, axis=0, keepdims=True)

    total = lax.fori_loop(0, tiles, total_turn, jnp.exp(pos - peak))
    log_total = peak + jnp.log(total)
    loss_ref[0] = (log_total - pos) * live
    pos_grad = (jnp.exp(pos - log_total) - 1.0) * live
    scale = jnp.exp(peak - log_total) * live
    query_grad_ref[...] = jnp.zeros_like(query_grad_ref)

    @pl.when(span == 0)
    def _():
        target_grad_ref[...] = jnp.zeros_like(target_grad_ref)

    def grad_turn(t, carried):
        rows = pl.ds(pl.multiple_of(t * tile, tile), tile)
        number = lax.broadcasted_iota(jnp.int32, (tile, 1), 0) + t * tile
        weight = score_ref[rows] * scale + jnp.where(target == number, pos_grad, 0.0)
        w0, w1 = split2(weight)
        t0, t1 = parts_ref[0, rows], parts_ref[1, rows]
        q0, q1 = query_parts_ref[0], query_parts_ref[1]
        query_grad_ref[...] += (mxu(w0, t1, TN) + mxu(w1, t0, TN)) + mxu(w0, t0, TN)
        target_grad_ref[rows] += (mxu(w0, q1, NN) + mxu(w1, q0, NN)) + mxu(w0, q0, NN)
        return carried

    lax.fori_loop(0, tiles, grad_turn, 0)


def span_step(edge_count, target, slots, queries, table):
    spans, negatives = slots.shape[0], slots.shape[2]
    table_rows = table.shape[0]
    f32 = jnp.float32
    return pl.pallas_call(
        span_kernel,
        grid=(spans,),
        in_specs=[
            pl.BlockSpec(memory_space=pltpu.SMEM),
            vmem((1, 1, SPAN), lambda i: (i, 0, 0)),
            vmem((1, 1, negatives), lambda i: (i, 0, 0)),
            vmem((SPAN, WIDE), lambda i: (i, 0)),
            vmem((table_rows, WIDE), lambda i: (0, 0)),
        ],
        out_specs=[
            vmem((1, 1, SPAN), lambda i: (i, 0, 0)),
            vmem((SPAN, WIDE), lambda i: (i, 0)),
            vmem((table_rows, WIDE), lambda i: (0, 0)),
        ],
        out_shape=[
            jax.ShapeDtypeStruct((spans, 1, SPAN), f32),
            jax.ShapeDtypeStruct((spans * SPAN, WIDE), f32),
            jax.ShapeDtypeStruct((table_rows, WIDE), f32),
        ],
        scratch_shapes=[
            pltpu.VMEM((table_rows, SPAN), f32),
            pltpu.VMEM((table_rows, 1), f32),
            pltpu.VMEM((3, table_rows, WIDE), jnp.bfloat16),
            pltpu.VMEM((3, SPAN, WIDE), jnp.bfloat16),
        ],
        compiler_params=params(),
        cost_estimate=pl.CostEstimate(
            flops=24 * spans * SPAN * table_rows * WIDE,
            bytes_accessed=16 * table_rows * WIDE,
            transcendentals=spans * SPAN * table_rows,
        ),
        name="span_step",
    )(edge_count, target, slots, queries, table)


def put_kernel(with_product, index_ref, value_ref, *rest):
    if with_product:
        other_ref, out_ref, parts_ref = rest
    else:
        out_ref, parts_ref = rest

    @pl.when(pl.program_id(0) == 0)
    def _():
        value = value_ref[...]
        if with_product:
            value = conj_product(value, other_ref[...])
        for k, part in enumerate(split2(value)):
            parts_ref[k] = part

    tile = out_ref.shape[0]
    rows = lax.broadcasted_iota(jnp.int32, (tile, index_ref.shape[1]), 0) + pl.program_id(0) * tile
    pick = jnp.where(rows == index_ref[...], 1.0, 0.0).astype(jnp.bfloat16)
    out_ref[...] = mxu(pick, parts_ref[1], NN) + mxu(pick, parts_ref[0], NN)


def put_rows(index, rows, value, other=None):
    count = value.shape[0]
    tile = min(256, rows)
    whole = vmem((count, WIDE), lambda i: (0, 0))
    operands = (index, value) if other is None else (index, value, other)
    return pl.pallas_call(
        functools.partial(put_kernel, other is not None),
        grid=(rows // tile,),
        in_specs=[vmem((1, count), lambda i: (0, 0))] + [whole] * (len(operands) - 1),
        out_specs=vmem((tile, WIDE), lambda i: (i, 0)),
        out_shape=jax.ShapeDtypeStruct((rows, WIDE), jnp.float32),
        scratch_shapes=[pltpu.VMEM((2, count, WIDE), jnp.bfloat16)],
        compiler_params=params(),
        cost_estimate=pl.CostEstimate(
            flops=4 * rows * count * WIDE, bytes_accessed=4 * (rows + count) * WIDE, transcendentals=0
        ),
        name="put_rows",
    )(*operands)


def passed_along(value, axis, by):
    count = lax.axis_size(axis)
    return lax.ppermute(value, axis, [(i, (i + by) % count) for i in range(count)])


def exchanged(value, axis):
    return lax.all_to_all(value, axis, split_axis=0, concat_axis=0, tiled=True)


def adagrad(params_, accumulator, gradient, width):
    new_state = accumulator + jnp.sum(gradient * gradient, axis=1) / width
    return params_ - LEARN_RATE * gradient / jnp.sqrt(new_state)[:, None]


def on_device(
    entity,
    entity_state,
    relation,
    relation_state,
    src_send,
    dst_send,
    edge_source,
    edge_relation,
    edge_target,
    neg_slots,
    edge_count,
):
    width = entity.shape[1]
    owned = entity.shape[0]
    relations = relation.shape[0]
    peers, block = src_send.shape[1], src_send.shape[2]
    table_rows = peers * block
    edges = edge_source.shape[0]
    spans = edges // SPAN
    groups, shards = lax.axis_size("group"), lax.axis_size("shard")
    share = -(-relations // (groups * shards))
    padded = share * groups * shards

    entity_wide = wide(entity)
    moved_index = passed_along(dst_send, "group", -1)
    moved_entity = passed_along(entity_wide, "group", -1)
    src_rows = take_rows(entity_wide, src_send.reshape(table_rows, 1))
    source_table = exchanged(src_rows.reshape(peers, block, WIDE), "shard").reshape(table_rows, WIDE)
    relation_wide = jnp.pad(wide(relation), ((0, padded - relations), (0, 0)))
    relation_state_wide = jnp.pad(relation_state, (0, padded - relations), constant_values=1.0)
    rels = take_rows(relation_wide, edge_relation.reshape(edges, 1))
    target_rows = take_rows(moved_entity, moved_index.reshape(table_rows, 1))
    target_table = exchanged(target_rows.reshape(peers, block, WIDE), "shard").reshape(table_rows, WIDE)
    heads, queries = make_queries(source_table, edge_source.reshape(edges, 1), rels)

    loss, query_grad, target_grad = span_step(
        edge_count,
        edge_target.reshape(spans, 1, SPAN),
        neg_slots.reshape(spans, 1, neg_slots.shape[1]),
        queries,
        target_table,
    )
    returned_target = exchanged(target_grad.reshape(peers, block, WIDE), "shard").reshape(table_rows, WIDE)

    relation_part = put_rows(edge_relation.reshape(1, edges), padded, query_grad, heads)
    relation_blocks = exchanged(relation_part.reshape(shards, groups * share, WIDE), "shard")
    relation_some = jnp.sum(relation_blocks, axis=0)
    relation_own = jnp.sum(exchanged(relation_some.reshape(groups, share, WIDE), "group"), axis=0)

    dense_grad = put_rows(moved_index.reshape(1, table_rows), owned, returned_target)
    moved_grad = passed_along(dense_grad, "group", 1)

    source_grad = put_rows(edge_source.reshape(1, edges), table_rows, query_grad, rels)
    returned_source = exchanged(source_grad.reshape(peers, block, WIDE), "shard").reshape(table_rows, WIDE)
    own_grad = put_rows(src_send.reshape(1, table_rows), owned, returned_source)

    first = (lax.axis_index("shard") * groups + lax.axis_index("group")) * share
    relation_mine = adagrad(
        lax.dynamic_slice_in_dim(relation_wide, first, share),
        lax.dynamic_slice_in_dim(relation_state_wide, first, share),
        relation_own,
        width,
    )
    relation_some_new = lax.all_gather(narrow(relation_mine, width), "group", axis=0, tiled=True)
    relation_new = lax.all_gather(relation_some_new, "shard", axis=0, tiled=True)[:relations]

    entity_grad = narrow(own_grad + moved_grad, width)
    entity_new = adagrad(entity, entity_state, entity_grad, width)
    return entity_new, relation_new, loss.reshape(edges)


def solution(mesh):
    return jax.shard_map(
        on_device,
        mesh=mesh,
        in_specs=(
            P(("group", "shard"), None),
            P(("group", "shard")),
            P(),
            P(),
            P(("group", "shard"), None, None),
            P(("group", "shard"), None, None),
            P(("group", "shard")),
            P(("group", "shard")),
            P(("group", "shard")),
            P(("group", "shard"), None),
            P(("group", "shard")),
        ),
        out_specs=(P(("group", "shard"), None), P(), P(("group", "shard"))),
        check_vma=False,
    )
```

time: 601 us -> 399 us (0.66)
  the two profiles are of different devices: /device:TPU:8 before, /device:TPU:7 now
where the time goes in v1:
time: 399 us
  waiting for transfers between devices  112 us (28%)
  blocking collectives  110 us (28%)
  starting transfers between devices  73.7 us (18%)
  Pallas kernels  58.4 us (15%)
  local copies, waits for them, and re-layouts  25 us (6%)
  between operations  15 us (4%)
  other arithmetic  4.42 us (1%)
    all_to_all x4, starting transfers between devices, exchanged(): return lax.all_to_all(value, axis, split_axis=0, concat_axis=0, tiled=True)  70.7 us
    all_to_all x2, blocking collectives, exchanged(): return lax.all_to_all(value, axis, split_axis=0, concat_axis=0, tiled=True)  60.7 us
    all_gather x1, waiting for transfers between devices, on_device(): lax.all_gather(relation_some_new, 'shard', axis=0, tiled=True)[:relations]  52.2 us
    all_gather x1, blocking collectives, on_device(): lax.all_gather(narrow(relation_mine, width), 'group', axis=0, tiled=True)  49.1 us
    ppermute x3, waiting for transfers between devices, passed_along(): lax.ppermute(value, axis, [(i, (i + by) % count) for i in range(count)])  40 us
    pallas_call x1, Pallas kernels, span_step(): pl.pallas_call(span_kernel, grid=(spans,), in_specs=[pl.BlockSpec(memory_...  21.9 us
    all_to_all x4, waiting for transfers between devices, exchanged(): return lax.all_to_all(value, axis, split_axis=0, concat_axis=0, tiled=True)  20 us
    unnamed x48, local copies, waits for them, and re-layouts  19.7 us
  transfers between devices with their start and end apart: 8, of which 5 were waited for; matrix products, arithmetic and copies ran while one was open for 3% of the time, Pallas kernels for 7%

profile of v1, /device:TPU:7, one launch (start us, length us, event | category | flops | bytes accessed | tf_op | source)
XLA Modules:
  0.0 398.6 jit_solution(13798434939479480781)
XLA Ops:
  10.3 3.7 take_rows.3
  14.0 6.6 %all-to-all-start = ((f32[16,64,512]{2,1,0:T(8,128)}), f32[16,64,512]{2,1,0:T(8,128)}, u32[]{:S(2)}, u32[]{:S(2)}) async-start(f32[16,64,512]{2,1,0:T(8,128)} %bitcast.3), calls=%async_computation | async-start | bytes 4194304 | tf_op jit(solution)/shard_map/all_to_all | solution.py:295
  21.4 26.9 %collective-permute-done = s32[1,16,64]{2,1,0:T(8,128)S(1)} collective-permute-done((s32[1,16,64]{2,1,0:T(8,128)S(1)}, s32[1,16,64]{2,1,0:T(8,128)S(1)}, u32[]{:S(2)}, u32[]{:S(2)}) %collective-permute-start) | collective-permute-done | bytes 4128 | tf_op jit(solution)/shard_map/ppermute | solution.py:291
  48.8 3.8 take_rows.5
  52.6 51.2 %all-to-all-start.1 = ((f32[16,64,512]{2,1,0:T(8,128)}), f32[16,64,512]{2,1,0:T(8,128)}, u32[]{:S(2)}, u32[]{:S(2)}) async-start(f32[16,64,512]{2,1,0:T(8,128)} %bitcast.6), calls=%async_computation.1 | async-start | bytes 4194304 | tf_op jit(solution)/shard_map/all_to_all | solution.py:295
  113.1 6.7 %take_rows.4.rel_ref.rest_0_ = f32[1024,512]{1,0:T(8,128)S(1)} custom-call(s32[1024,1]{1,0:T(8,128)S(1)} %copy.37.index_ref, f32[1536,512]{1,0:T(8,128)S(1)} %pad.26.table_ref), custom_call_target="tpu_custom_call" | custom-call | flops 4831838208 | bytes 5242880 | tf_op jit(solution)/shard_map/take_rows/pallas_call | solution.py:87
  121.1 6.6 %make_queries.1 = (f32[1024,512]{1,0:T(8,128)S(1)}, f32[1024,512]{1,0:T(8,128)S(1)}) custom-call(s32[1024,1]{1,0:T(8,128)S(1)} %copy.38.index_ref, f32[1024,512]{1,0:T(8,128)} %bitcast.4.table_ref, f32[1024,512]{1,0:T(8,128)} %copy-done.5), custom_call_target="tpu_custom_call" | custom-call | flops 3221225472 | bytes 10485760 | tf_op jit(solution)/shard_map/make_queries/pallas_call | solution.py:119
  131.6 21.9 %span_step.1 = (f32[2,1,512]{2,1,0:T(1,128)}, f32[1024,512]{1,0:T(8,128)S(1)}, f32[1024,512]{1,0:T(8,128)S(1)}) custom-call(s32[1]{0:T(128)S(6)} %copy.45.count_ref, s32[2,1,512]{2,1,0:T(1,128)S(1)} %bitcast.24, s32[2,1,1000]{2,1,0:T(1,128)S(1)} %reshape.74.slots_ref, f32[1024,512]{1,0:T(8,128)} %copy-done.10, f32[1024,512]{1,0:T(8,128)} %bitcast.7.table_ref), custom_call_target="tpu_custom_call" | custom-call | flops 12884901888 | bytes 8388608 | tf_op jit(solution)/shard_map/span_step/pallas_call | solution.py:213
  154.8 5.8 %put_rows.7 = f32[1536,512]{1,0:T(8,128)} custom-call(s32[1,1024]{1,0:T(1,128)S(1)} %bitcast.21, f32[1024,512]{1,0:T(8,128)S(1)} %get-tuple-element.9.value_ref, f32[1024,512]{1,0:T(8,128)S(1)} %copy-done.9), custom_call_target="tpu_custom_call" | custom-call | flops 3221225472 | bytes 5242880 | tf_op jit(solution)/shard_map/put_rows/pallas_call | solution.py:274
  160.6 44.0 %all_to_all.30 = f32[16,96,512]{2,1,0:T(8,128)S(1)} all-to-all(f32[16,96,512]{2,1,0:T(8,128)} %bitcast.25), channel_id=1, replica_groups=mesh['group'=16,'shard'=16] {'shard'}, dimensions={0} | all-to-all | bytes 6291456 | tf_op jit(solution)/shard_map/all_to_all | solution.py:295
  204.9 16.7 %all_to_all.31 = f32[16,6,512]{2,1,0:T(8,128)S(1)} all-to-all(f32[16,6,512]{2,1,0:T(8,128)S(1)} %reshape.90), channel_id=1, replica_groups=mesh['group'=16,'shard'=16] {'group'}, dimensions={0} | all-to-all | bytes 393216 | tf_op jit(solution)/shard_map/all_to_all | solution.py:295
  221.6 6.8 %all-to-all-start.3 = ((f32[16,64,512]{2,1,0:T(8,128)}), f32[16,64,512]{2,1,0:T(8,128)S(1)}, u32[]{:S(2)}, u32[]{:S(2)}) async-start(f32[16,64,512]{2,1,0:T(8,128)} %bitcast.18), calls=%async_computation.3 | async-start | bytes 4194304 | tf_op jit(solution)/shard_map/all_to_all | solution.py:295
  228.4 1.6 copy-done.7
  230.0 4.9 %put_rows.4 = f32[1024,512]{1,0:T(8,128)S(1)} custom-call(s32[1,1024]{1,0:T(1,128)S(1)} %bitcast.23, f32[1024,512]{1,0:T(8,128)S(1)} %copy-done.7, f32[1024,512]{1,0:T(8,128)} %copy-done.5), custom_call_target="tpu_custom_call" | custom-call | flops 2147483648 | bytes 4194304 | tf_op jit(solution)/shard_map/put_rows/pallas_call | solution.py:274
  237.4 18.8 %all-to-all-done.3 = f32[16,64,512]{2,1,0:T(8,128)S(1)} async-done(((f32[16,64,512]{2,1,0:T(8,128)}), f32[16,64,512]{2,1,0:T(8,128)S(1)}, u32[]{:S(2)}, u32[]{:S(2)}) %all-to-all-start.3) | async-done | bytes 2097184 | tf_op jit(solution)/shard_map/all_to_all | solution.py:295
  256.2 6.0 %all-to-all-start.2 = ((f32[16,64,512]{2,1,0:T(8,128)}), f32[16,64,512]{2,1,0:T(8,128)}, u32[]{:S(2)}, u32[]{:S(2)}) async-start(f32[16,64,512]{2,1,0:T(8,128)} %bitcast.19), calls=%async_computation.2 | async-start | bytes 4194304 | tf_op jit(solution)/shard_map/all_to_all | solution.py:295
  262.3 49.1 %all-gather = f32[16,6,400]{2,1,0:T(8,128)S(1)} all-gather(f32[1,6,400]{2,1,0:T(8,128)S(1)} %maximum_bitcast_fusion), channel_id=1, replica_groups=mesh['group'=16,'shard'=16] {'group'}, dimensions={0}, use_global_device_ids=true | all-gather | bytes 163200 | tf_op jit(solution)/shard_map/all_gather | solution.py:367
  312.2 1.7 put_rows.6
  314.0 2.2 collective-permute-start.2
  316.2 3.3 put_rows.5
  319.6 13.1 %collective-permute-done.2 = f32[512,512]{1,0:T(8,128)S(1)} collective-permute-done((f32[512,512]{1,0:T(8,128)S(1)}, f32[512,512]{1,0:T(8,128)S(1)}, u32[]{:S(2)}, u32[]{:S(2)}) %collective-permute-start.2) | collective-permute-done | bytes 1048608 | tf_op jit(solution)/shard_map/ppermute | solution.py:291
  335.7 52.2 %all-gather.3.cloned.1.call-done = f32[1536,400]{1,0:T(8,128)} async-done(((f32[96,400]{1,0:T(8,128)}), f32[1536,400]{1,0:T(8,128)}) %all-gather.3.cloned.1.call-update) | async-done | bytes 2457616 | tf_op jit(solution)/shard_map/all_gather | solution.py:368
  387.9 1.8 slice-done
  389.7 2.1 copy.42
  (85 shorter events, 26.0 us)
Async XLA Ops:
  7.2 1.7 copy-start.18
  7.2 2.5 copy-start.15
  14.0 7.2 %copy-start.20 = (s32[1,16,64]{2,1,0:T(8,128)S(1)}, s32[1,16,64]{2,1,0:T(8,128)}, u32[]{:S(2)}) copy-start(s32[1,16,64]{2,1,0:T(8,128)} %param.16) | copy-start | bytes 12292
  14.0 38.7 %all-to-all-start = ((f32[16,64,512]{2,1,0:T(8,128)}), f32[16,64,512]{2,1,0:T(8,128)}, u32[]{:S(2)}, u32[]{:S(2)}) async-start(f32[16,64,512]{2,1,0:T(8,128)} %bitcast.3), calls=%async_computation | async-start | bytes 4194304 | tf_op jit(solution)/shard_map/all_to_all | solution.py:295
  20.6 28.2 %collective-permute-start.1 = (f32[512,512]{1,0:T(8,128)S(1)}, f32[512,512]{1,0:T(8,128)S(1)}, u32[]{:S(2)}, u32[]{:S(2)}) collective-permute-start(f32[512,512]{1,0:T(8,128)S(1)} %select_maximum_fusion.1.table_ref), channel_id=1, source_target_pairs={{0,240},{16,0},{32,16},{48,32},{64,48},{80,64},{96,80},{112,96},{1... | collective-permute-start | bytes 3145736 | tf_op jit(solution)/shard_map/ppermute | solution.py:291
  21.2 27.2 %collective-permute-start = (s32[1,16,64]{2,1,0:T(8,128)S(1)}, s32[1,16,64]{2,1,0:T(8,128)S(1)}, u32[]{:S(2)}, u32[]{:S(2)}) collective-permute-start(s32[1,16,64]{2,1,0:T(8,128)S(1)} %copy-done.20), channel_id=1, source_target_pairs={{0,240},{16,0},{32,16},{48,32},{64,48},{80,64},{96,80},{112,96},{1... | collective-permute-start | bytes 12296 | tf_op jit(solution)/shard_map/ppermute | solution.py:291
  52.6 78.9 %all-to-all-start.1 = ((f32[16,64,512]{2,1,0:T(8,128)}), f32[16,64,512]{2,1,0:T(8,128)}, u32[]{:S(2)}, u32[]{:S(2)}) async-start(f32[16,64,512]{2,1,0:T(8,128)} %bitcast.6), calls=%async_computation.1 | async-start | bytes 4194304 | tf_op jit(solution)/shard_map/all_to_all | solution.py:295
  103.9 1.4 slice-start.1
  103.9 2.9 slice-start.2
  105.2 3.0 copy-start.2
  106.8 1.7 copy-start.3
  106.8 2.0 copy-start.17
  108.3 2.6 copy-start.14
  111.3 1.5 copy-start.11
  121.1 10.5 %copy-start.4 = (s32[1024]{0:T(1024)S(1)}, s32[1024]{0:T(1024)}, u32[]{:S(2)}) copy-start(s32[1024]{0:T(1024)} %param.19) | copy-start | bytes 12292
  131.6 23.2 %copy-start.9 = (f32[1024,512]{1,0:T(8,128)S(1)}, f32[1024,512]{1,0:T(8,128)}, u32[]{:S(2)}) copy-start(f32[1024,512]{1,0:T(8,128)} %copy-done.8) | copy-start | bytes 6291460
  154.8 5.8 %copy-start.6 = (f32[1024,512]{1,0:T(8,128)}, f32[1024,512]{1,0:T(8,128)S(1)}, u32[]{:S(2)}) copy-start(f32[1024,512]{1,0:T(8,128)S(1)} %get-tuple-element.9.value_ref) | copy-start | bytes 6291460
  221.6 34.5 %all-to-all-start.3 = ((f32[16,64,512]{2,1,0:T(8,128)}), f32[16,64,512]{2,1,0:T(8,128)S(1)}, u32[]{:S(2)}, u32[]{:S(2)}) async-start(f32[16,64,512]{2,1,0:T(8,128)} %bitcast.18), calls=%async_computation.3 | async-start | bytes 4194304 | tf_op jit(solution)/shard_map/all_to_all | solution.py:295
  228.4 1.6 copy-start.7
  230.0 6.4 %copy-start.16 = (f32[1345]{0:T(1024)S(1)}, f32[1345]{0:T(1024)}, u32[]{:S(2)}) copy-start(f32[1345]{0:T(1024)} %param.14) | copy-start | bytes 16144
  256.2 60.1 %all-to-all-start.2 = ((f32[16,64,512]{2,1,0:T(8,128)}), f32[16,64,512]{2,1,0:T(8,128)}, u32[]{:S(2)}, u32[]{:S(2)}) async-start(f32[16,64,512]{2,1,0:T(8,128)} %bitcast.19), calls=%async_computation.2 | async-start | bytes 4194304 | tf_op jit(solution)/shard_map/all_to_all | solution.py:295
  262.2 125.7 %all-gather.3.cloned.1.call-start = ((), (), s32[]{:S(2)}) async-start(), calls=%async_computation.6 | async-start | bytes 3342336 | tf_op jit(solution)/shard_map/all_gather | solution.py:368
  314.0 18.7 %collective-permute-start.2 = (f32[512,512]{1,0:T(8,128)S(1)}, f32[512,512]{1,0:T(8,128)S(1)}, u32[]{:S(2)}, u32[]{:S(2)}) collective-permute-start(f32[512,512]{1,0:T(8,128)S(1)} %put_rows.6), channel_id=1, source_target_pairs={{0,16},{16,32},{32,48},{48,64},{64,80},{80,96},{96,112},{112,128},... | collective-permute-start | bytes 3145736 | tf_op jit(solution)/shard_map/ppermute | solution.py:291
  387.9 1.8 slice-start
  (8 other events, 9.6 us)
Sparse Core Ops, SparseCore 0:
  312.3 75.5 all-gather.2

commit v2 on v1

--- a/solution.py
+++ b/solution.py
@@ -9,8 +9,9 @@
 
 SPAN = 512
 LEARN_RATE = 0.5
-HALF = 256
-WIDE = 2 * HALF
+WIDE = 512
+TAIL = 8
+MESH = pl.DeviceIdType.MESH
 
 NT = (((1,), (1,)), ((), ()))
 NN = (((1,), (0,)), ((), ()))
@@ -37,23 +38,60 @@
 
 def wide(x):
     half = x.shape[1] // 2
-    pad = ((0, 0), (0, HALF - half))
-    return jnp.concatenate([jnp.pad(x[:, :half], pad), jnp.pad(x[:, half:], pad)], axis=1)
+    re, im = x[:, :half], x[:, half:]
+    zeros = jnp.zeros((x.shape[0], WIDE - x.shape[1]), x.dtype)
+    return jnp.concatenate(
+        [re[:, :128], im[:, :128], re[:, 128:192], im[:, 128:192], re[:, 192:], im[:, 192:], zeros], axis=1
+    )
 
 
 def narrow(x, width):
-    half = width // 2
-    return jnp.concatenate([x[:, :half], x[:, HALF : HALF + half]], axis=1)
+    tail = width // 2 - 192
+    return jnp.concatenate(
+        [
+            x[:, :128], x[:, 256:320], x[:, 384 : 384 + tail],
+            x[:, 128:256], x[:, 320:384], x[:, 384 + tail : 384 + 2 * tail],
+        ],
+        axis=1,
+    )
+
+
+def swapped(x, half):
+    lane = lax.broadcasted_iota(jnp.int32, x.shape, 1)
+    if half == 64:
+        return pltpu.roll(x, 64, 1), lane < half
+    left, right = pltpu.roll(x, 128 - half, 1), pltpu.roll(x, half, 1)
+    mixed = jnp.where(lane < half, left, jnp.where(lane < 2 * half, right, 0.0))
+    return mixed, lane < half
+
+
+def mixed_product(a, b, half, sign):
+    other_a, low = swapped(a, half)
+    other_b, _ = swapped(b, half)
+    real = jnp.where(low, b, other_b)
+    imag = jnp.where(low, -other_b, b)
+    return a * real + sign * (other_a * imag)
+
+
+def product_of(a, b, sign):
+    ar, ai, br, bi = a[:, :128], a[:, 128:256], b[:, :128], b[:, 128:256]
+    return jnp.concatenate(
+        [
+            ar * br - sign * (ai * bi),
+            ai * br + sign * (ar * bi),
+            mixed_product(a[:, 256:384], b[:, 256:384], 64, sign),
+            mixed_product(a[:, 384:], b[:, 384:], TAIL, sign),
+        ],
+        axis=1,
+    )
 
 
 def product(a, b):
-    ar, ai, br, bi = a[:, :HALF], a[:, HALF:], b[:, :HALF], b[:, HALF:]
-    return jnp.concatenate([ar * br - ai * bi, ar * bi + ai * br], axis=1)
+    return product_of(a, b, 1.0)
 
 
 def conj_product(a, b):
-    ar, ai, br, bi = a[:, :HALF], a[:, HALF:], b[:, :HALF], b[:, HALF:]
-    return jnp.concatenate([ar * br + ai * bi, ai * br - ar * bi], axis=1)
+    return product_of(a, b, -1.0)
 
 
 def chosen(index, count):
@@ -268,7 +306,7 @@
 
 def put_rows(index, rows, value, other=None):
     count = value.shape[0]
-    tile = min(256, rows)
+    tile = next(t for t in (256, 176, 128, 64, 32, 16, 8) if rows % t == 0)
     whole = vmem((count, WIDE), lambda i: (0, 0))
     operands = (index, value) if other is None else (index, value, other)
     return pl.pallas_call(
@@ -286,6 +324,398 @@
     )(*operands)
 
 
+def pack_tail(x):
+    rows = x.shape[0]
+    packed = []
+    for first in range(0, rows, 64):
+        total = x[first : first + 8]
+        for k in range(1, min(8, (rows - first) // 8)):
+            total = total + pltpu.roll(x[first + 8 * k : first + 8 * k + 8], 16 * k, 1)
+        packed.append(total)
+    return packed[0] if len(packed) == 1 else jnp.concatenate(packed, axis=0)
+
+
+def unpack_tail(x, rows):
+    lane = lax.broadcasted_iota(jnp.int32, (8, 128), 1)
+    tiles = []
+    for t in range(rows // 8):
+        part = x[8 * (t // 8) : 8 * (t // 8) + 8]
+        k = t % 8
+        part = part if k == 0 else pltpu.roll(part, 128 - 16 * k, 1)
+        tiles.append(jnp.where(lane < 16, part, 0.0))
+    return tiles[0] if len(tiles) == 1 else jnp.concatenate(tiles, axis=0)
+
+
+def packed_rows(rows):
+    return 3 * rows + 8 * (-(-rows // 64))
+
+
+def store_packed(ref, x):
+    n = x.shape[0]
+    for c in range(3):
+        ref[c * n : (c + 1) * n] = x[:, 128 * c : 128 * c + 128]
+    ref[3 * n :] = pack_tail(x[:, 384:])
+
+
+def load_packed(ref, n):
+    parts = [ref[c * n : (c + 1) * n] for c in range(3)]
+    return parts, unpack_tail(ref[3 * n :], n)
+
+
+def remote(src, dst, send, recv, **device):
+    return pltpu.make_async_remote_copy(
+        src_ref=src, dst_ref=dst, send_sem=send, recv_sem=recv, device_id=device, device_id_type=MESH
+    )
+
+
+def greet(shards, groups, shard, group):
+    barrier = pltpu.get_barrier_semaphore()
+
+    def near(k, carried):
+        pl.semaphore_signal(
+            barrier, inc=1, device_id={"shard": lax.rem(shard + k, shards)}, device_id_type=MESH
+        )
+        return carried
+
+    def far(k, carried):
+        pl.semaphore_signal(
+            barrier, inc=1, device_id={"group": lax.rem(group + k, groups)}, device_id_type=MESH
+        )
+        return carried
+
+    lax.fori_loop(1, shards, near, 0)
+    lax.fori_loop(1, groups, far, 0)
+    pl.semaphore_wait(barrier, shards + groups - 2)
+
+
+def back_kernel(
+    sizes,
+    target_ref, source_ref, part_ref, relation_ref, relation_state_ref,
+    moved_index_ref, source_index_ref, entity_ref, entity_state_ref,
+    entity_new_ref, relation_new_ref,
+    tsend, trecv, ssend, srecv, dense, moved, pick, values,
+    r0send, r0recv, r1, r1recv, r2, r2recv, r3, r3recv, r4, r5,
+    t_s, t_r, s_s, s_r, p_s, p_r, r0_s, r0_r, r1_s, r1_r, r2_s, r2_r, r3_s, r3_r, r4_s, r4_r, r5_s, r5_r,
+):
+    shards, groups, block, owned, width = sizes
+    chips = shards // 2
+    shard, group = lax.axis_index("shard"), lax.axis_index("group")
+    core, chip = lax.rem(shard, 2), lax.div(shard, 2)
+    partner = shard + 1 - 2 * core
+    after = lax.rem(group + 1, groups)
+    rb = part_ref.shape[0] // shards
+    piece = r2.shape[1]
+    stages = ((0, block), (block, block), (2 * block, packed_rows(block) - 2 * block))
+    moves = ((0, owned), (owned, owned), (2 * owned, packed_rows(owned) - 2 * owned))
+
+    greet(shards, groups, shard, group)
+
+    def pack_target(p, carried):
+        rows = pl.ds(pl.multiple_of(p * block, block), block)
+        store_packed(tsend.at[p], target_ref[rows])
+        return carried
+
+    lax.fori_loop(0, shards, pack_target, 0)
+
+    def target_copy(stage, to, slot):
+        first, size = stages[stage]
+        rows = pl.ds(first, size)
+        return remote(
+            tsend.at[to, rows], trecv.at[slot, rows], t_s.at[stage, to], t_r.at[stage, slot], shard=to
+        )
+
+    for stage in range(3):
+        def send_target(k, carried, stage=stage):
+            to = lax.rem(shard + k, shards)
+            target_copy(stage, to, shard).start()
+            return carried
+
+        lax.fori_loop(1, shards, send_target, 0)
+
+    def half_block(which, q):
+        return pl.ds(pl.multiple_of((which * chips + q) * rb, rb), rb)
+
+    def pack_other(q, carried):
+        store_packed(r0send.at[q], part_ref[half_block(1 - core, q)])
+        return carried
+
+    lax.fori_loop(0, chips, pack_other, 0)
+    pair = remote(r0send, r0recv, r0_s, r0_r, shard=partner)
+    pair.start()
+
+    def pack_own(q, carried):
+        store_packed(r1.at[q], part_ref[half_block(core, q)])
+        return carried
+
+    lax.fori_loop(0, chips, pack_own, 0)
+    trecv[shard] = tsend[shard]
+    pair.wait_recv()
+
+    def add_pair(q, carried):
+        r1[q] = r1[q] + r0recv[q]
+        return carried
+
+    lax.fori_loop(0, chips, add_pair, 0)
+
+    def chip_copy(to, slot):
+        return remote(r1.at[to], r1recv.at[slot], r1_s.at[to], r1_r.at[slot], shard=2 * to + core)
+
+    def send_chip(k, carried):
+        chip_copy(lax.rem(chip + k, chips), chip).start()
+        return carried
+
+    lax.fori_loop(1, chips, send_chip, 0)
+
+    def pack_source(p, carried):
+        rows = pl.ds(pl.multiple_of(p * block, block), block)
+        store_packed(ssend.at[p], source_ref[rows])
+        return carried
+
+    lax.fori_loop(0, shards, pack_source, 0)
+
+    def source_copy(to, slot):
+        return remote(ssend.at[to], srecv.at[slot], s_s.at[to], s_r.at[slot], shard=to)
+
+    def send_source(k, carried):
+        source_copy(lax.rem(shard + k, shards), shard).start()
+        return carried
+
+    lax.fori_loop(1, shards, send_source, 0)
+    srecv[shard] = ssend[shard]
+
+    number = lax.broadcasted_iota(jnp.int32, (owned, 1), 0)
+    pick[...] = jnp.where(number == moved_index_ref[...], 1.0, 0.0).astype(jnp.bfloat16)
+
+    def placed(value):
+        v0, v1 = split2(value)
+        return mxu(pick[...], v1, NN) + mxu(pick[...], v0, NN)
+
+    def tails(ref):
+        def turn(p, carried):
+            values[pl.ds(pl.multiple_of(p * block, block), block)] = unpack_tail(ref[p, 3 * block :], block)
+            return carried
+
+        lax.fori_loop(0, shards, turn, 0)
+        return values[...]
+
+    def move(stage):
+        first, size = moves[stage]
+        rows = pl.ds(first, size)
+        return remote(dense.at[rows], moved.at[rows], p_s.at[stage], p_r.at[stage], group=after)
+
+    for stage in range(3):
+        def wait_target(k, carried, stage=stage):
+            frm = lax.rem(shard + k, shards)
+            target_copy(stage, frm, frm).wait_recv()
+            return carried
+
+        lax.fori_loop(1, shards, wait_target, 0)
+        chunk = trecv[:, stage * block : (stage + 1) * block].reshape(shards * block, 128)
+        dense[stage * owned : (stage + 1) * owned] = placed(chunk)
+        if stage == 2:
+            dense[3 * owned :] = pack_tail(placed(tails(trecv)))
+        move(stage).start()
+
+    r2[...] = jnp.zeros_like(r2)
+
+    def wait_chip(k, carried):
+        frm = lax.rem(chip + k, chips)
+        chip_copy(frm, frm).wait_recv()
+        return carried
+
+    lax.fori_loop(1, chips, wait_chip, 0)
+    r1recv[chip] = r1[chip]
+    total = r1recv[0]
+    for q in range(1, chips):
+        total = total + r1recv[q]
+    size = total.shape[0]
+    for h in range(groups):
+        count = min(piece, size - h * piece)
+        if count > 0:
+            r2[h, :count] = total[h * piece : h * piece + count]
+
+    def group_copy(to, slot):
+        return remote(r2.at[to], r2recv.at[slot], r2_s.at[to], r2_r.at[slot], group=to)
+
+    def send_group(k, carried):
+        group_copy(lax.rem(group + k, groups), group).start()
+        return carried
+
+    def wait_group(k, carried):
+        frm = lax.rem(group + k, groups)
+        group_copy(frm, frm).wait_recv()
+        return carried
+
+    lax.fori_loop(1, groups, send_group, 0)
+    r2recv[group] = r2[group]
+    lax.fori_loop(1, groups, wait_group, 0)
+    r3[...] = jnp.sum(r2recv[...], axis=0)
+
+    def share_copy(to, slot):
+        return remote(r3, r3recv.at[slot], r3_s.at[to], r3_r.at[slot], group=to)
+
+    def send_share(k, carried):
+        share_copy(lax.rem(group + k, groups), group).start()
+        return carried
+
+    def wait_share(k, carried):
+        frm = lax.rem(group + k, groups)
+        share_copy(frm, frm).wait_recv()
+        return carried
+
+    lax.fori_loop(1, groups, send_share, 0)
+    r3recv[group] = r3[...]
+    lax.fori_loop(1, groups, wait_share, 0)
+
+    def updated(param_ref, rows, state, gradient):
+        squares = sum(jnp.sum(g * g, axis=1, keepdims=True) for g in gradient)
+        root = jnp.sqrt(state + squares / width)
+        return [
+            param_ref[rows, 128 * c : 128 * c + 128] - LEARN_RATE * g / root for c, g in enumerate(gradient)
+        ]
+
+    summed = r3recv[...].reshape(groups * piece, 128)
+    gradient = [summed[c * rb : (c + 1) * rb] for c in range(3)]
+    gradient.append(unpack_tail(summed[3 * rb : size], rb))
+    mine = half_block(core, chip)
+    fresh = updated(relation_ref, mine, relation_state_ref[mine], gradient)
+    store_packed(r4.at[chip], jnp.concatenate(fresh, axis=1))
+
+    def spread_copy(to, slot):
+        return remote(r4.at[chip], r4.at[chip], r4_s.at[to], r4_r.at[chip], shard=2 * to + core)
+
+    def spread_wait(frm):
+        return remote(r4.at[frm], r4.at[frm], r4_s.at[frm], r4_r.at[frm], shard=2 * frm + core)
+
+    def hand_copy(q):
+        return remote(r4.at[q], r5.at[q], r5_s.at[q], r5_r.at[q], shard=partner)
+
+    def send_spread(k, carried):
+        spread_copy(lax.rem(chip + k, chips), chip).start()
+        return carried
+
+    lax.fori_loop(1, chips, send_spread, 0)
+    hand_copy(chip).start()
+
+    def wait_source(k, carried):
+        frm = lax.rem(shard + k, shards)
+        source_copy(frm, frm).wait_recv()
+        return carried
+
+    lax.fori_loop(1, shards, wait_source, 0)
+    pick[...] = jnp.where(number == source_index_ref[...], 1.0, 0.0).astype(jnp.bfloat16)
+    own = []
+    for c in range(3):
+        own.append(placed(srecv[:, c * block : (c + 1) * block].reshape(shards * block, 128)))
+    own.append(placed(tails(srecv)))
+    for c in range(4):
+        entity_new_ref[:, 128 * c : 128 * c + 128] = own[c]
+    for stage in range(3):
+        move(stage).wait_recv()
+    parts, tail = load_packed(moved, owned)
+    parts.append(tail)
+    gradient = [entity_new_ref[:, 128 * c : 128 * c + 128] + parts[c] for c in range(4)]
+    fresh = updated(entity_ref, slice(None), entity_state_ref[...], gradient)
+    for c in range(4):
+        entity_new_ref[:, 128 * c : 128 * c + 128] = fresh[c]
+
+    def forward(k, carried):
+        frm = lax.rem(chip + k, chips)
+        spread_wait(frm).wait_recv()
+        hand_copy(frm).start()
+        return carried
+
+    lax.fori_loop(1, chips, forward, 0)
+
+    def put_out(which, ref):
+        def turn(q, carried):
+            rows = half_block(which, q)
+            got, tail_ = load_packed(ref.at[q], rb)
+            for c in range(3):
+                relation_new_ref[rows, 128 * c : 128 * c + 128] = got[c]
+            relation_new_ref[rows, 384:] = tail_
+            return carried
+
+        lax.fori_loop(0, chips, turn, 0)
+
+    put_out(core, r4)
+
+    def take_hand(q, carried):
+        hand_copy(q).wait_recv()
+        return carried
+
+    lax.fori_loop(0, chips, take_hand, 0)
+    put_out(1 - core, r5)
+
+    for stage in range(3):
+        def end_target(k, carried, stage=stage):
+            to = lax.rem(shard + k, shards)
+            target_copy(stage, to, shard).wait_send()
+            return carried
+
+        lax.fori_loop(1, shards, end_target, 0)
+        move(stage).wait_send()
+
+    def end_shard(k, carried):
+        source_copy(lax.rem(shard + k, shards), shard).wait_send()
+        return carried
+
+    def end_chip(k, carried):
+        to = lax.rem(chip + k, chips)
+        chip_copy(to, chip).wait_send()
+        spread_copy(to, chip).wait_send()
+        return carried
+
+    def end_group(k, carried):
+        to = lax.rem(group + k, groups)
+        group_copy(to, group).wait_send()
+        share_copy(to, group).wait_send()
+        return carried
+
+    def end_hand(q, carried):
+        hand_copy(q).wait_send()
+        return carried
+
+    lax.fori_loop(1, shards, end_shard, 0)
+    lax.fori_loop(1, chips, end_chip, 0)
+    lax.fori_loop(1, groups, end_group, 0)
+    lax.fori_loop(0, chips, end_hand, 0)
+    pair.wait_send()
+
+
+def back_step(sizes, *operands):
+    shards, groups, block, owned, width = sizes
+    padded = operands[2].shape[0]
+    chips, rb = shards // 2, padded // shards
+    size = packed_rows(rb)
+    piece = 8 * (-(-size // (8 * groups)))
+    f32 = jnp.float32
+    table = pltpu.VMEM((shards, packed_rows(block), 128), f32)
+    flat = pltpu.VMEM((packed_rows(owned), 128), f32)
+    half = pltpu.VMEM((chips, size, 128), f32)
+    pieces = pltpu.VMEM((groups, piece, 128), f32)
+    dma = pltpu.SemaphoreType.DMA
+    return pl.pallas_call(
+        functools.partial(back_kernel, sizes),
+        in_specs=[pl.BlockSpec(memory_space=pltpu.VMEM)] * len(operands),
+        out_specs=[pl.BlockSpec(memory_space=pltpu.VMEM)] * 2,
+        out_shape=[jax.ShapeDtypeStruct((owned, WIDE), f32), jax.ShapeDtypeStruct((padded, WIDE), f32)],
+        scratch_shapes=[
+            table, table, table, table, flat, flat,
+            pltpu.VMEM((owned, shards * block), jnp.bfloat16),
+            pltpu.VMEM((shards * block, 128), f32),
+            half, half, half, half, pieces, pieces, pltpu.VMEM((piece, 128), f32), pieces, half, half,
+            dma((3, shards)), dma((3, shards)), dma((shards,)), dma((shards,)), dma((3,)), dma((3,)),
+            dma, dma, dma((chips,)), dma((chips,)), dma((groups,)), dma((groups,)),
+            dma((groups,)), dma((groups,)), dma((chips,)), dma((chips,)), dma((chips,)), dma((chips,)),
+        ],
+        compiler_params=pltpu.CompilerParams(
+            collective_id=1, has_side_effects=True, vmem_limit_bytes=60 << 20
+        ),
+        name="back_step",
+    )(*operands)
+
+
 def passed_along(value, axis, by):
     count = lax.axis_size(axis)
     return lax.ppermute(value, axis, [(i, (i + by) % count) for i in range(count)])
@@ -293,11 +723,6 @@
 
 def exchanged(value, axis):
     return lax.all_to_all(value, axis, split_axis=0, concat_axis=0, tiled=True)
-
-
-def adagrad(params_, accumulator, gradient, width):
-    new_state = accumulator + jnp.sum(gradient * gradient, axis=1) / width
-    return params_ - LEARN_RATE * gradient / jnp.sqrt(new_state)[:, None]
 
 
 def on_device(
@@ -321,8 +746,7 @@
     edges = edge_source.shape[0]
     spans = edges // SPAN
     groups, shards = lax.axis_size("group"), lax.axis_size("shard")
-    share = -(-relations // (groups * shards))
-    padded = share * groups * shards
+    padded = 8 * shards * (-(-relations // (8 * shards)))
 
     entity_wide = wide(entity)
     moved_index = passed_along(dst_send, "group", -1)
@@ -330,7 +754,7 @@
     src_rows = take_rows(entity_wide, src_send.reshape(table_rows, 1))
     source_table = exchanged(src_rows.reshape(peers, block, WIDE), "shard").reshape(table_rows, WIDE)
     relation_wide = jnp.pad(wide(relation), ((0, padded - relations), (0, 0)))
-    relation_state_wide = jnp.pad(relation_state, (0, padded - relations), constant_values=1.0)
+    relation_state_wide = jnp.pad(relation_state[:, None], ((0, padded - relations), (0, 0)), constant_values=1.0)
     rels = take_rows(relation_wide, edge_relation.reshape(edges, 1))
     target_rows = take_rows(moved_entity, moved_index.reshape(table_rows, 1))
     target_table = exchanged(target_rows.reshape(peers, block, WIDE), "shard").reshape(table_rows, WIDE)
@@ -343,33 +767,21 @@
         queries,
         target_table,
     )
-    returned_target = exchanged(target_grad.reshape(peers, block, WIDE), "shard").reshape(table_rows, WIDE)
-
     relation_part = put_rows(edge_relation.reshape(1, edges), padded, query_grad, heads)
-    relation_blocks = exchanged(relation_part.reshape(shards, groups * share, WIDE), "shard")
-    relation_some = jnp.sum(relation_blocks, axis=0)
-    relation_own = jnp.sum(exchanged(relation_some.reshape(groups, share, WIDE), "group"), axis=0)
-
-    dense_grad = put_rows(moved_index.reshape(1, table_rows), owned, returned_target)
-    moved_grad = passed_along(dense_grad, "group", 1)
-
     source_grad = put_rows(edge_source.reshape(1, edges), table_rows, query_grad, rels)
-    returned_source = exchanged(source_grad.reshape(peers, block, WIDE), "shard").reshape(table_rows, WIDE)
-    own_grad = put_rows(src_send.reshape(1, table_rows), owned, returned_source)
-
-    first = (lax.axis_index("shard") * groups + lax.axis_index("group")) * share
-    relation_mine = adagrad(
-        lax.dynamic_slice_in_dim(relation_wide, first, share),
-        lax.dynamic_slice_in_dim(relation_state_wide, first, share),
-        relation_own,
-        width,
+    entity_new, relation_new = back_step(
+        (shards, groups, block, owned, width),
+        target_grad,
+        source_grad,
+        relation_part,
+        relation_wide,
+        relation_state_wide,
+        moved_index.reshape(1, table_rows),
+        src_send.reshape(1, table_rows),
+        entity_wide,
+        entity_state.reshape(owned, 1),
     )
-    relation_some_new = lax.all_gather(narrow(relation_mine, width), "group", axis=0, tiled=True)
-    relation_new = lax.all_gather(relation_some_new, "shard", axis=0, tiled=True)[:relations]
-
-    entity_grad = narrow(own_grad + moved_grad, width)
-    entity_new = adagrad(entity, entity_state, entity_grad, width)
-    return entity_new, relation_new, loss.reshape(edges)
+    return narrow(entity_new, width), narrow(relation_new[:relations], width), loss.reshape(edges)
 
 
 def solution(mesh):

time: 399 us -> 335 us (0.84)
  the two profiles are of different devices: /device:TPU:7 before, /device:TPU:57 now
where the time goes in v2:
time: 335 us; the launch traced here: 334 us
  Pallas kernels  197 us (59%)
  waiting for transfers between devices  60.2 us (18%)
  local copies, waits for them, and re-layouts  54 us (16%)
  starting transfers between devices  21.3 us (6%)
    pallas_call x1, Pallas kernels, back_step(): pl.pallas_call(functools.partial(back_kernel, sizes), in_specs=[pl.BlockS...  141 us
    ppermute x2, waiting for transfers between devices, passed_along(): lax.ppermute(value, axis, [(i, (i + by) % count) for i in range(count)])  60.2 us
    pallas_call x1, Pallas kernels, span_step(): pl.pallas_call(span_kernel, grid=(spans,), in_specs=[pl.BlockSpec(memory_...  21.8 us
    pallas_call x3, Pallas kernels, take_rows(): pl.pallas_call(take_kernel, grid=(rows // tile,), in_specs=[vmem((tile, 1...  14 us
    pallas_call x2, Pallas kernels, put_rows(): pl.pallas_call(functools.partial(put_kernel, other is not None), grid=(ro...  13.9 us
    all_to_all x2, starting transfers between devices, exchanged(): return lax.all_to_all(value, axis, split_axis=0, concat_axis=0, tiled=True)  13.4 us
    unnamed x46, local copies, waits for them, and re-layouts  12.6 us
    ppermute x2, starting transfers between devices, passed_along(): lax.ppermute(value, axis, [(i, (i + by) % count) for i in range(count)])  7.82 us
  transfers between devices with their start and end apart: 4, of which 1 were waited for; matrix products, arithmetic and copies ran while one was open for 7% of the time, Pallas kernels for 5%

profile of v2, /device:TPU:57, one launch (start us, length us, event | category | flops | bytes accessed | tf_op | source)
XLA Modules:
  0.0 334.2 jit_solution(5397309081188884586)
XLA Ops:
  5.4 3.7 %take_rows.3 = f32[1024,512]{1,0:T(8,128)} custom-call(s32[1024,1]{1,0:T(8,128)S(1)} %reshape.70.index_ref, f32[512,512]{1,0:T(8,128)S(1)} %concatenate.12.table_ref.entity_ref), custom_call_target="tpu_custom_call" | custom-call | flops 1610612736 | bytes 3145728 | tf_op jit(solution)/shard_map/take_rows/pallas_call | solution.py:125
  9.1 6.1 %all-to-all-start = ((f32[16,64,512]{2,1,0:T(8,128)}), f32[16,64,512]{2,1,0:T(8,128)}, u32[]{:S(2)}, u32[]{:S(2)}) async-start(f32[16,64,512]{2,1,0:T(8,128)} %bitcast.2), calls=%async_computation | async-start | bytes 4194304 | tf_op jit(solution)/shard_map/all_to_all | solution.py:725
  15.2 7.3 %collective-permute-start.1 = (f32[512,512]{1,0:T(8,128)S(1)}, f32[512,512]{1,0:T(8,128)S(1)}, u32[]{:S(2)}, u32[]{:S(2)}) collective-permute-start(f32[512,512]{1,0:T(8,128)S(1)} %concatenate.12.table_ref.entity_ref), channel_id=1, source_target_pairs={{0,240},{16,0},{32,16},{48,32},{64,48},{80,64},{96,80},{112,96},{1... | collective-permute-start | bytes 3145736 | tf_op jit(solution)/shard_map/ppermute | solution.py:721
  23.1 60.2 %collective-permute-done = s32[1,16,64]{2,1,0:T(8,128)S(1)} collective-permute-done((s32[1,16,64]{2,1,0:T(8,128)S(1)}, s32[1,16,64]{2,1,0:T(8,128)S(1)}, u32[]{:S(2)}, u32[]{:S(2)}) %collective-permute-start) | collective-permute-done | bytes 4128 | tf_op jit(solution)/shard_map/ppermute | solution.py:721
  83.7 3.7 %take_rows.5 = f32[1024,512]{1,0:T(8,128)} custom-call(s32[1024,1]{1,0:T(8,128)S(1)} %reshape.71.index_ref, f32[512,512]{1,0:T(8,128)S(1)} %collective-permute-done.1.table_ref), custom_call_target="tpu_custom_call" | custom-call | flops 1610612736 | bytes 3145728 | tf_op jit(solution)/shard_map/take_rows/pallas_call | solution.py:125
  87.4 7.3 %all-to-all-start.1 = ((f32[16,64,512]{2,1,0:T(8,128)}), f32[16,64,512]{2,1,0:T(8,128)}, u32[]{:S(2)}, u32[]{:S(2)}) async-start(f32[16,64,512]{2,1,0:T(8,128)} %bitcast.5), calls=%async_computation.1 | async-start | bytes 4194304 | tf_op jit(solution)/shard_map/all_to_all | solution.py:725
  95.4 1.4 fusion.5
  99.0 1.4 fusion.3
  103.5 5.4 %concatenate.13 = f32[1345,512]{1,0:T(8,128)} concatenate(f32[1345,128]{1,0:T(8,128)S(1)} %copy.52, f32[1345,128]{1,0:T(8,128)S(1)} %copy.53, f32[1345,64]{1,0:T(8,128)S(1)} %copy.54, f32[1345,64]{1,0:T(8,128)S(1)} %copy.55, f32[1345,8]{1,0:T(8,128)S(1)} %copy.39, f32[1345,8]{1,0:T(8,128)} %copy.40, f32[1345,112]{1,0:T(8,128)} %broadcast_in_dim.10), dimensions={1} | concatenate | bytes 5509120 | tf_op jit(solution)/shard_map/concatenate | solution.py:43
  108.9 2.1 pad.8.table_ref.relation_ref
  115.1 2.0 pad.9.relation_state_ref
  118.2 6.5 %take_rows.4.rel_ref.rest_0_ = f32[1024,512]{1,0:T(8,128)S(1)} custom-call(s32[1024,1]{1,0:T(8,128)S(1)} %copy-done.4, f32[1408,512]{1,0:T(8,128)S(1)} %pad.8.table_ref.relation_ref), custom_call_target="tpu_custom_call" | custom-call | flops 4429185024 | bytes 4980736 | tf_op jit(solution)/shard_map/take_rows/pallas_call | solution.py:125
  126.7 6.9 %make_queries.1 = (f32[1024,512]{1,0:T(8,128)S(1)}, f32[1024,512]{1,0:T(8,128)S(1)}) custom-call(s32[1024,1]{1,0:T(8,128)S(1)} %copy.42.index_ref, f32[1024,512]{1,0:T(8,128)} %bitcast.3.table_ref, f32[1024,512]{1,0:T(8,128)} %copy-done.8), custom_call_target="tpu_custom_call" | custom-call | flops 3221225472 | bytes 10485760 | tf_op jit(solution)/shard_map/make_queries/pallas_call | solution.py:157
  133.7 1.4 copy-done.9
  136.5 21.8 %span_step.1 = (f32[2,1,512]{2,1,0:T(1,128)}, f32[1024,512]{1,0:T(8,128)S(1)}, f32[1024,512]{1,0:T(8,128)S(1)}) custom-call(s32[1]{0:T(128)S(6)} %copy.56.count_ref, s32[2,1,512]{2,1,0:T(1,128)S(1)} %bitcast.15, s32[2,1,1000]{2,1,0:T(1,128)S(1)} %reshape.55.slots_ref, f32[1024,512]{1,0:T(8,128)} %copy-done.11, f32[1024,512]{1,0:T(8,128)} %bitcast.6.table_ref), custom_call_target="tpu_custom_call" | custom-call | flops 12884901888 | bytes 8388608 | tf_op jit(solution)/shard_map/span_step/pallas_call | solution.py:251
  159.6 6.3 %put_rows.2.source_ref = f32[1024,512]{1,0:T(8,128)S(1)} custom-call(s32[1,1024]{1,0:T(1,128)S(1)} %bitcast.12, f32[1024,512]{1,0:T(8,128)S(1)} %get-tuple-element.12.value_ref, f32[1024,512]{1,0:T(8,128)} %copy-done.8), custom_call_target="tpu_custom_call" | custom-call | flops 2147483648 | bytes 4194304 | tf_op jit(solution)/shard_map/put_rows/pallas_call | solution.py:312
  167.3 7.6 %put_rows.3.part_ref = f32[1408,512]{1,0:T(8,128)} custom-call(s32[1,1024]{1,0:T(1,128)S(1)} %bitcast.14, f32[1024,512]{1,0:T(8,128)S(1)} %get-tuple-element.12.value_ref, f32[1024,512]{1,0:T(8,128)S(1)} %copy-done.10), custom_call_target="tpu_custom_call" | custom-call | flops 2952790016 | bytes 4980736 | tf_op jit(solution)/shard_map/put_rows/pallas_call | solution.py:312
  174.8 140.6 %back_step.1 = (f32[512,512]{1,0:T(8,128)}, f32[1408,512]{1,0:T(8,128)}) custom-call(f32[1024,512]{1,0:T(8,128)} %copy-done.2, f32[1024,512]{1,0:T(8,128)} %copy-done.3, f32[1408,512]{1,0:T(8,128)} %put_rows.3.part_ref, f32[1408,512]{1,0:T(8,128)} %copy-done, f32[1408,1]{1,0:T(8,128)} %pad.9.relation_state_ref, s32[1,1024]{1,0:T(1,128)} %reshape.66.moved_index_ref, ...), custom_call_target="tpu_custom_call" | custom-call | tf_op jit(solution)/shard_map/back_step/pallas_call | solution.py:698
  315.4 2.4 fusion
  317.8 2.7 fusion.1
  320.5 2.5 fusion.2
  325.6 3.6 %concatenate.15 = f32[1345,400]{1,0:T(8,128)S(1)} concatenate(f32[1345,128]{1,0:T(8,128)} %get-tuple-element.28, f32[1345,64]{1,0:T(8,128)} %get-tuple-element.26, f32[1345,8]{1,0:T(8,128)} %get-tuple-element.24, f32[1345,128]{1,0:T(8,128)} %get-tuple-element.27, f32[1345,64]{1,0:T(8,128)} %get-tuple-element.25, f32[1345,8]{1,0:T(8,128)S(1)} %get-tuple-element.23), dimensions={1} | concatenate | bytes 4304000 | tf_op jit(solution)/shard_map/concatenate | solution.py:50
  329.1 2.1 copy.47
  331.2 1.8 concatenate.14
  (71 shorter events, 25.8 us)
Async XLA Ops:
  0.6 3.6 %copy-start.13 = (s32[1,16,64]{2,1,0:T(8,128)S(1)}, s32[1,16,64]{2,1,0:T(8,128)}, u32[]{:S(2)}) copy-start(s32[1,16,64]{2,1,0:T(8,128)} %param.15) | copy-start | bytes 12292
  5.4 9.9 %copy-start.1 = (f32[512,512]{1,0:T(8,128)}, f32[512,512]{1,0:T(8,128)S(1)}, u32[]{:S(2)}) copy-start(f32[512,512]{1,0:T(8,128)S(1)} %concatenate.12.table_ref.entity_ref) | copy-start | bytes 3145732
  9.1 13.4 %copy-start.17 = (s32[1,16,64]{2,1,0:T(8,128)S(1)}, s32[1,16,64]{2,1,0:T(8,128)}, u32[]{:S(2)}) copy-start(s32[1,16,64]{2,1,0:T(8,128)} %param.16) | copy-start | bytes 12292
  9.1 78.3 %all-to-all-start = ((f32[16,64,512]{2,1,0:T(8,128)}), f32[16,64,512]{2,1,0:T(8,128)}, u32[]{:S(2)}, u32[]{:S(2)}) async-start(f32[16,64,512]{2,1,0:T(8,128)} %bitcast.2), calls=%async_computation | async-start | bytes 4194304 | tf_op jit(solution)/shard_map/all_to_all | solution.py:725
  15.2 68.5 %collective-permute-start.1 = (f32[512,512]{1,0:T(8,128)S(1)}, f32[512,512]{1,0:T(8,128)S(1)}, u32[]{:S(2)}, u32[]{:S(2)}) collective-permute-start(f32[512,512]{1,0:T(8,128)S(1)} %concatenate.12.table_ref.entity_ref), channel_id=1, source_target_pairs={{0,240},{16,0},{32,16},{48,32},{64,48},{80,64},{96,80},{112,96},{1... | collective-permute-start | bytes 3145736 | tf_op jit(solution)/shard_map/ppermute | solution.py:721
  22.5 60.7 %collective-permute-start = (s32[1,16,64]{2,1,0:T(8,128)S(1)}, s32[1,16,64]{2,1,0:T(8,128)S(1)}, u32[]{:S(2)}, u32[]{:S(2)}) collective-permute-start(s32[1,16,64]{2,1,0:T(8,128)S(1)} %copy-done.17), channel_id=1, source_target_pairs={{0,240},{16,0},{32,16},{48,32},{64,48},{80,64},{96,80},{112,96},{1... | collective-permute-start | bytes 12296 | tf_op jit(solution)/shard_map/ppermute | solution.py:721
  87.4 49.0 %all-to-all-start.1 = ((f32[16,64,512]{2,1,0:T(8,128)}), f32[16,64,512]{2,1,0:T(8,128)}, u32[]{:S(2)}, u32[]{:S(2)}) async-start(f32[16,64,512]{2,1,0:T(8,128)} %bitcast.5), calls=%async_computation.1 | async-start | bytes 4194304 | tf_op jit(solution)/shard_map/all_to_all | solution.py:725
  108.9 2.1 copy-start.6
  108.9 3.4 %copy-start.5 = (s32[1024]{0:T(1024)S(1)}, s32[1024]{0:T(1024)}, u32[]{:S(2)}) copy-start(s32[1024]{0:T(1024)} %param.17) | copy-start | bytes 12292
  108.9 3.6 %copy-start.15 = (s32[2,1000]{1,0:T(2,128)S(1)}, s32[2,1000]{1,0:T(2,128)}, u32[]{:S(2)}) copy-start(s32[2,1000]{1,0:T(2,128)} %param.20) | copy-start | bytes 24004
  108.9 4.3 %copy-start.14 = (f32[1345]{0:T(1024)S(1)}, f32[1345]{0:T(1024)}, u32[]{:S(2)}) copy-start(f32[1345]{0:T(1024)} %param.14) | copy-start | bytes 16144
  108.9 5.4 %copy-start.16 = (f32[512]{0:T(512)S(1)}, f32[512]{0:T(512)}, u32[]{:S(2)}) copy-start(f32[512]{0:T(512)} %param.12) | copy-start | bytes 6148
  111.0 13.7 %copy-start = (f32[1408,512]{1,0:T(8,128)}, f32[1408,512]{1,0:T(8,128)S(1)}, u32[]{:S(2)}) copy-start(f32[1408,512]{1,0:T(8,128)S(1)} %pad.8.table_ref.relation_ref) | copy-start | bytes 8650756
  117.1 1.0 copy-start.4
  124.7 1.3 copy-start.8
  126.7 9.8 %copy-start.7 = (s32[1024]{0:T(1024)S(1)}, s32[1024]{0:T(1024)}, u32[]{:S(2)}) copy-start(s32[1024]{0:T(1024)} %param.19) | copy-start | bytes 12292
  133.7 1.4 copy-start.9
  135.1 1.4 copy-start.11
  158.3 1.3 copy-start.2
  159.6 7.7 %copy-start.10 = (f32[1024,512]{1,0:T(8,128)S(1)}, f32[1024,512]{1,0:T(8,128)}, u32[]{:S(2)}) copy-start(f32[1024,512]{1,0:T(8,128)} %copy-done.9) | copy-start | bytes 6291460
  165.9 1.3 copy-start.3
  317.8 5.2 %copy-start.12 = (f32[512,512]{1,0:T(8,128)S(1)}, f32[512,512]{1,0:T(8,128)}, u32[]{:S(2)}) copy-start(f32[512,512]{1,0:T(8,128)} %get-tuple-element.14) | copy-start | bytes 3145732

commit v3 on v2

--- a/solution.py
+++ b/solution.py
@@ -36,24 +36,46 @@
     return lax.dot_general(a, b, dims, preferred_element_type=jnp.float32)
 
 
-def wide(x):
-    half = x.shape[1] // 2
-    re, im = x[:, :half], x[:, half:]
-    zeros = jnp.zeros((x.shape[0], WIDE - x.shape[1]), x.dtype)
-    return jnp.concatenate(
-        [re[:, :128], im[:, :128], re[:, 128:192], im[:, 128:192], re[:, 192:], im[:, 192:], zeros], axis=1
+def lane_of(x):
+    return lax.broadcasted_iota(jnp.int32, x.shape, 1)
+
+
+def widened(x0, x1, x2, x3):
+    lane = lane_of(x0)
+    imag = jnp.where(lane < 56, pltpu.roll(x1, 56, 1), pltpu.roll(x2, 56, 1))
+    both = jnp.where(
+        lane < 64, x1, jnp.where(lane < 120, pltpu.roll(x2, 120, 1), pltpu.roll(x3, 120, 1))
     )
-
-
-def narrow(x, width):
-    tail = width // 2 - 192
-    return jnp.concatenate(
-        [
-            x[:, :128], x[:, 256:320], x[:, 384 : 384 + tail],
-            x[:, 128:256], x[:, 320:384], x[:, 384 + tail : 384 + 2 * tail],
-        ],
-        axis=1,
-    )
+    tail = jnp.where(lane < 8, pltpu.roll(x1, 64, 1), jnp.where(lane < 16, x3, 0.0))
+    return x0, imag, both, tail
+
+
+def narrowed(real, imag, both, tail):
+    lane = lane_of(real)
+    imag_on, both_on = pltpu.roll(imag, 72, 1), pltpu.roll(both, 8, 1)
+    x1 = jnp.where(lane < 64, both, jnp.where(lane < 72, pltpu.roll(tail, 64, 1), imag_on))
+    x2 = jnp.where(lane < 72, imag_on, both_on)
+    return real, x1, x2, jnp.where(lane < 8, both_on, tail)
+
+
+def load_wide(ref, rows, count, last):
+    last[:count] = jnp.zeros((count, 128), jnp.float32)
+    last[:count, :16] = ref[rows, 384:400]
+    return widened(ref[rows, 0:128], ref[rows, 128:256], ref[rows, 256:384], last[:count])
+
+
+def store_narrow(ref, rows, parts):
+    x = narrowed(*parts)
+    for c in range(3):
+        ref[rows, 128 * c : 128 * c + 128] = x[c]
+    ref[rows, 384:400] = x[3][:, :16]
+
+
+def column_of(row_ref, first, count):
+    n = row_ref.shape[1]
+    lane = lax.broadcasted_iota(jnp.int32, (count, n), 1)
+    own = lax.broadcasted_iota(jnp.int32, (count, n), 0) + first
+    return jnp.sum(jnp.where(lane == own, row_ref[...], 0.0), axis=1, keepdims=True)
 
 
 def swapped(x, half):
@@ -94,9 +116,9 @@
     return product_of(a, b, -1.0)
 
 
-def chosen(index, count):
-    lanes = lax.broadcasted_iota(jnp.int32, (index.shape[0], count), 1)
-    return jnp.where(lanes == index, 1.0, 0.0).astype(jnp.bfloat16)
+def picked(index, count):
+    rows = lax.broadcasted_iota(jnp.int32, (count, index.shape[1]), 0)
+    return jnp.where(rows == index, 1.0, 0.0).astype(jnp.bfloat16)
 
 
 def vmem(shape, index_map):
@@ -105,68 +127,6 @@
 
 def params(limit=48 << 20):
     return pltpu.CompilerParams(vmem_limit_bytes=limit)
-
-
-def take_kernel(index_ref, table_ref, out_ref, parts_ref):
-    @pl.when(pl.program_id(0) == 0)
-    def _():
-        for k, part in enumerate(split3(table_ref[...])):
-            parts_ref[k] = part
-
-    pick = chosen(index_ref[...], table_ref.shape[0])
-    out_ref[...] = (
-        mxu(pick, parts_ref[0], NN) + mxu(pick, parts_ref[1], NN)
-    ) + mxu(pick, parts_ref[2], NN)
-
-
-def take_rows(table, index):
-    rows, count = index.shape[0], table.shape[0]
-    tile = min(256, rows)
-    return pl.pallas_call(
-        take_kernel,
-        grid=(rows // tile,),
-        in_specs=[vmem((tile, 1), lambda i: (i, 0)), vmem((count, WIDE), lambda i: (0, 0))],
-        out_specs=vmem((tile, WIDE), lambda i: (i, 0)),
-        out_shape=jax.ShapeDtypeStruct((rows, WIDE), jnp.float32),
-        scratch_shapes=[pltpu.VMEM((3, count, WIDE), jnp.bfloat16)],
-        compiler_params=params(),
-        cost_estimate=pl.CostEstimate(
-            flops=6 * rows * count * WIDE, bytes_accessed=4 * (rows + count) * WIDE, transcendentals=0
-        ),
-        name="take_rows",
-    )(index, table)
-
-
-def query_kernel(index_ref, table_ref, rel_ref, head_ref, query_ref, parts_ref):
-    @pl.when(pl.program_id(0) == 0)
-    def _():
-        for k, part in enumerate(split3(table_ref[...])):
-            parts_ref[k] = part
-
-    pick = chosen(index_ref[...], table_ref.shape[0])
-    heads = (mxu(pick, parts_ref[0], NN) + mxu(pick, parts_ref[1], NN)) + mxu(pick, parts_ref[2], NN)
-    head_ref[...] = heads
-    query_ref[...] = product(heads, rel_ref[...])
-
-
-def make_queries(table, index, rels):
-    rows, count = index.shape[0], table.shape[0]
-    tile = min(256, rows)
-    block = vmem((tile, WIDE), lambda i: (i, 0))
-    shape = jax.ShapeDtypeStruct((rows, WIDE), jnp.float32)
-    return pl.pallas_call(
-        query_kernel,
-        grid=(rows // tile,),
-        in_specs=[vmem((tile, 1), lambda i: (i, 0)), vmem((count, WIDE), lambda i: (0, 0)), block],
-        out_specs=[block, block],
-        out_shape=[shape, shape],
-        scratch_shapes=[pltpu.VMEM((3, count, WIDE), jnp.bfloat16)],
-        compiler_params=params(),
-        cost_estimate=pl.CostEstimate(
-            flops=6 * rows * count * WIDE, bytes_accessed=4 * (4 * rows + count) * WIDE, transcendentals=0
-        ),
-        name="make_queries",
-    )(index, table, rels)
 
 
 def span_kernel(
@@ -284,46 +244,6 @@
     )(edge_count, target, slots, queries, table)
 
 
-def put_kernel(with_product, index_ref, value_ref, *rest):
-    if with_product:
-        other_ref, out_ref, parts_ref = rest
-    else:
-        out_ref, parts_ref = rest
-
-    @pl.when(pl.program_id(0) == 0)
-    def _():
-        value = value_ref[...]
-        if with_product:
-            value = conj_product(value, other_ref[...])
-        for k, part in enumerate(split2(value)):
-            parts_ref[k] = part
-
-    tile = out_ref.shape[0]
-    rows = lax.broadcasted_iota(jnp.int32, (tile, index_ref.shape[1]), 0) + pl.program_id(0) * tile
-    pick = jnp.where(rows == index_ref[...], 1.0, 0.0).astype(jnp.bfloat16)
-    out_ref[...] = mxu(pick, parts_ref[1], NN) + mxu(pick, parts_ref[0], NN)
-
-
-def put_rows(index, rows, value, other=None):
-    count = value.shape[0]
-    tile = next(t for t in (256, 176, 128, 64, 32, 16, 8) if rows % t == 0)
-    whole = vmem((count, WIDE), lambda i: (0, 0))
-    operands = (index, value) if other is None else (index, value, other)
-    return pl.pallas_call(
-        functools.partial(put_kernel, other is not None),
-        grid=(rows // tile,),
-        in_specs=[vmem((1, count), lambda i: (0, 0))] + [whole] * (len(operands) - 1),
-        out_specs=vmem((tile, WIDE), lambda i: (i, 0)),
-        out_shape=jax.ShapeDtypeStruct((rows, WIDE), jnp.float32),
-        scratch_shapes=[pltpu.VMEM((2, count, WIDE), jnp.bfloat16)],
-        compiler_params=params(),
-        cost_estimate=pl.CostEstimate(
-            flops=4 * rows * count * WIDE, bytes_accessed=4 * (rows + count) * WIDE, transcendentals=0
-        ),
-        name="put_rows",
-    )(*operands)
-
-
 def pack_tail(x):
     rows = x.shape[0]
     packed = []
@@ -390,10 +310,10 @@
 
 def back_kernel(
     sizes,
-    target_ref, source_ref, part_ref, relation_ref, relation_state_ref,
-    moved_index_ref, source_index_ref, entity_ref, entity_state_ref,
+    target_ref, query_grad_ref, heads_ref, rels_ref, edge_source_ref, edge_relation_ref,
+    relation_ref, relation_state_ref, moved_index_ref, source_index_ref, entity_ref, entity_state_ref,
     entity_new_ref, relation_new_ref,
-    tsend, trecv, ssend, srecv, dense, moved, pick, values,
+    tsend, trecv, ssend, srecv, dense, moved, pick, values, grads, part_ref, last, dense_own,
     r0send, r0recv, r1, r1recv, r2, r2recv, r3, r3recv, r4, r5,
     t_s, t_r, s_s, s_r, p_s, p_r, r0_s, r0_r, r1_s, r1_r, r2_s, r2_r, r3_s, r3_r, r4_s, r4_r, r5_s, r5_r,
 ):
@@ -432,8 +352,39 @@
 
         lax.fori_loop(1, shards, send_target, 0)
 
+    edges = query_grad_ref.shape[0]
+    padded = part_ref.shape[0]
+    tile = 256
+    half_rows = padded // 2
+    put_tile = half_rows // 2 if half_rows % 32 == 0 else half_rows
+
     def half_block(which, q):
         return pl.ds(pl.multiple_of((which * chips + q) * rb, rb), rb)
+
+    def gradient_parts(other_ref):
+        def turn(t, carried):
+            rows = pl.ds(pl.multiple_of(t * tile, tile), tile)
+            for k, part in enumerate(split2(conj_product(query_grad_ref[rows], other_ref[rows]))):
+                grads[k, rows] = part
+            return carried
+
+        lax.fori_loop(0, edges // tile, turn, 0)
+
+    def summed_rows(index_ref, first, count):
+        number = lax.broadcasted_iota(jnp.int32, (count, edges), 0) + first
+        ones = jnp.where(number == index_ref[...], 1.0, 0.0).astype(jnp.bfloat16)
+        return mxu(ones, grads[1], NN) + mxu(ones, grads[0], NN)
+
+    def half_sums(which):
+        def turn(t, carried):
+            first = pl.multiple_of(which * half_rows + t * put_tile, put_tile)
+            part_ref[pl.ds(first, put_tile)] = summed_rows(edge_relation_ref, first, put_tile)
+            return carried
+
+        lax.fori_loop(0, half_rows // put_tile, turn, 0)
+
+    gradient_parts(heads_ref)
+    half_sums(1 - core)
 
     def pack_other(q, carried):
         store_packed(r0send.at[q], part_ref[half_block(1 - core, q)])
@@ -442,6 +393,7 @@
     lax.fori_loop(0, chips, pack_other, 0)
     pair = remote(r0send, r0recv, r0_s, r0_r, shard=partner)
     pair.start()
+    half_sums(core)
 
     def pack_own(q, carried):
         store_packed(r1.at[q], part_ref[half_block(core, q)])
@@ -449,42 +401,7 @@
 
     lax.fori_loop(0, chips, pack_own, 0)
     trecv[shard] = tsend[shard]
-    pair.wait_recv()
-
-    def add_pair(q, carried):
-        r1[q] = r1[q] + r0recv[q]
-        return carried
-
-    lax.fori_loop(0, chips, add_pair, 0)
-
-    def chip_copy(to, slot):
-        return remote(r1.at[to], r1recv.at[slot], r1_s.at[to], r1_r.at[slot], shard=2 * to + core)
-
-    def send_chip(k, carried):
-        chip_copy(lax.rem(chip + k, chips), chip).start()
-        return carried
-
-    lax.fori_loop(1, chips, send_chip, 0)
-
-    def pack_source(p, carried):
-        rows = pl.ds(pl.multiple_of(p * block, block), block)
-        store_packed(ssend.at[p], source_ref[rows])
-        return carried
-
-    lax.fori_loop(0, shards, pack_source, 0)
-
-    def source_copy(to, slot):
-        return remote(ssend.at[to], srecv.at[slot], s_s.at[to], s_r.at[slot], shard=to)
-
-    def send_source(k, carried):
-        source_copy(lax.rem(shard + k, shards), shard).start()
-        return carried
-
-    lax.fori_loop(1, shards, send_source, 0)
-    srecv[shard] = ssend[shard]
-
-    number = lax.broadcasted_iota(jnp.int32, (owned, 1), 0)
-    pick[...] = jnp.where(number == moved_index_ref[...], 1.0, 0.0).astype(jnp.bfloat16)
+    pick[...] = picked(moved_index_ref[...], owned)
 
     def placed(value):
         v0, v1 = split2(value)
@@ -503,8 +420,8 @@
         rows = pl.ds(first, size)
         return remote(dense.at[rows], moved.at[rows], p_s.at[stage], p_r.at[stage], group=after)
 
-    for stage in range(3):
-        def wait_target(k, carried, stage=stage):
+    def pass_on(stage):
+        def wait_target(k, carried):
             frm = lax.rem(shard + k, shards)
             target_copy(stage, frm, frm).wait_recv()
             return carried
@@ -515,6 +432,46 @@
         if stage == 2:
             dense[3 * owned :] = pack_tail(placed(tails(trecv)))
         move(stage).start()
+
+    pass_on(0)
+    pair.wait_recv()
+
+    def add_pair(q, carried):
+        r1[q] = r1[q] + r0recv[q]
+        return carried
+
+    lax.fori_loop(0, chips, add_pair, 0)
+
+    def chip_copy(to, slot):
+        return remote(r1.at[to], r1recv.at[slot], r1_s.at[to], r1_r.at[slot], shard=2 * to + core)
+
+    def send_chip(k, carried):
+        chip_copy(lax.rem(chip + k, chips), chip).start()
+        return carried
+
+    lax.fori_loop(1, chips, send_chip, 0)
+    pass_on(1)
+
+    gradient_parts(rels_ref)
+
+    def put_source(t, carried):
+        value = summed_rows(edge_source_ref, t * tile, tile)
+        for j in range(tile // block):
+            store_packed(ssend.at[t * (tile // block) + j], value[j * block : (j + 1) * block])
+        return carried
+
+    lax.fori_loop(0, shards * block // tile, put_source, 0)
+
+    def source_copy(to, slot):
+        return remote(ssend.at[to], srecv.at[slot], s_s.at[to], s_r.at[slot], shard=to)
+
+    def send_source(k, carried):
+        source_copy(lax.rem(shard + k, shards), shard).start()
+        return carried
+
+    lax.fori_loop(1, shards, send_source, 0)
+    srecv[shard] = ssend[shard]
+    pass_on(2)
 
     r2[...] = jnp.zeros_like(r2)
 
@@ -567,18 +524,16 @@
     r3recv[group] = r3[...]
     lax.fori_loop(1, groups, wait_share, 0)
 
-    def updated(param_ref, rows, state, gradient):
+    def updated(params_, state, gradient):
         squares = sum(jnp.sum(g * g, axis=1, keepdims=True) for g in gradient)
         root = jnp.sqrt(state + squares / width)
-        return [
-            param_ref[rows, 128 * c : 128 * c + 128] - LEARN_RATE * g / root for c, g in enumerate(gradient)
-        ]
+        return [p - LEARN_RATE * g / root for p, g in zip(params_, gradient)]
 
     summed = r3recv[...].reshape(groups * piece, 128)
     gradient = [summed[c * rb : (c + 1) * rb] for c in range(3)]
     gradient.append(unpack_tail(summed[3 * rb : size], rb))
-    mine = half_block(core, chip)
-    fresh = updated(relation_ref, mine, relation_state_ref[mine], gradient)
+    state = column_of(relation_state_ref, (core * chips + chip) * rb, rb)
+    fresh = updated(load_wide(relation_ref, half_block(core, chip), rb, last), state, gradient)
     store_packed(r4.at[chip], jnp.concatenate(fresh, axis=1))
 
     def spread_copy(to, slot):
@@ -603,21 +558,18 @@
         return carried
 
     lax.fori_loop(1, shards, wait_source, 0)
-    pick[...] = jnp.where(number == source_index_ref[...], 1.0, 0.0).astype(jnp.bfloat16)
-    own = []
+    pick[...] = picked(source_index_ref[...], owned)
     for c in range(3):
-        own.append(placed(srecv[:, c * block : (c + 1) * block].reshape(shards * block, 128)))
-    own.append(placed(tails(srecv)))
-    for c in range(4):
-        entity_new_ref[:, 128 * c : 128 * c + 128] = own[c]
+        dense_own[c] = placed(srecv[:, c * block : (c + 1) * block].reshape(shards * block, 128))
+    dense_own[3] = placed(tails(srecv))
     for stage in range(3):
         move(stage).wait_recv()
     parts, tail = load_packed(moved, owned)
     parts.append(tail)
-    gradient = [entity_new_ref[:, 128 * c : 128 * c + 128] + parts[c] for c in range(4)]
-    fresh = updated(entity_ref, slice(None), entity_state_ref[...], gradient)
-    for c in range(4):
-        entity_new_ref[:, 128 * c : 128 * c + 128] = fresh[c]
+    gradient = [dense_own[c] + parts[c] for c in range(4)]
+    entity_wide = load_wide(entity_ref, slice(None), owned, last)
+    fresh = updated(entity_wide, column_of(entity_state_ref, 0, owned), gradient)
+    store_narrow(entity_new_ref, slice(None), fresh)
 
     def forward(k, carried):
         frm = lax.rem(chip + k, chips)
@@ -629,11 +581,8 @@
 
     def put_out(which, ref):
         def turn(q, carried):
-            rows = half_block(which, q)
             got, tail_ = load_packed(ref.at[q], rb)
-            for c in range(3):
-                relation_new_ref[rows, 128 * c : 128 * c + 128] = got[c]
-            relation_new_ref[rows, 384:] = tail_
+            store_narrow(relation_new_ref, half_block(which, q), (*got, tail_))
             return carried
 
         lax.fori_loop(0, chips, turn, 0)
@@ -685,7 +634,8 @@
 
 def back_step(sizes, *operands):
     shards, groups, block, owned, width = sizes
-    padded = operands[2].shape[0]
+    padded = operands[6].shape[0]
+    edges = operands[1].shape[0]
     chips, rb = shards // 2, padded // shards
     size = packed_rows(rb)
     piece = 8 * (-(-size // (8 * groups)))
@@ -699,11 +649,15 @@
         functools.partial(back_kernel, sizes),
         in_specs=[pl.BlockSpec(memory_space=pltpu.VMEM)] * len(operands),
         out_specs=[pl.BlockSpec(memory_space=pltpu.VMEM)] * 2,
-        out_shape=[jax.ShapeDtypeStruct((owned, WIDE), f32), jax.ShapeDtypeStruct((padded, WIDE), f32)],
+        out_shape=[jax.ShapeDtypeStruct((owned, width), f32), jax.ShapeDtypeStruct((padded, width), f32)],
         scratch_shapes=[
             table, table, table, table, flat, flat,
             pltpu.VMEM((owned, shards * block), jnp.bfloat16),
             pltpu.VMEM((shards * block, 128), f32),
+            pltpu.VMEM((2, edges, WIDE), jnp.bfloat16),
+            pltpu.VMEM((padded, WIDE), f32),
+            pltpu.VMEM((owned, 128), f32),
+            pltpu.VMEM((4, owned, 128), f32),
             half, half, half, half, pieces, pieces, pltpu.VMEM((piece, 128), f32), pieces, half, half,
             dma((3, shards)), dma((3, shards)), dma((shards,)), dma((shards,)), dma((3,)), dma((3,)),
             dma, dma, dma((chips,)), dma((chips,)), dma((groups,)), dma((groups,)),
@@ -716,13 +670,213 @@
     )(*operands)
 
 
-def passed_along(value, axis, by):
-    count = lax.axis_size(axis)
-    return lax.ppermute(value, axis, [(i, (i + by) % count) for i in range(count)])
-
-
-def exchanged(value, axis):
-    return lax.all_to_all(value, axis, split_axis=0, concat_axis=0, tiled=True)
+def front_kernel(
+    sizes,
+    entity_ref, relation_ref, source_index_ref, target_index_ref, edge_source_ref, edge_relation_ref,
+    table_ref, heads_ref, rels_ref, queries_ref, moved_index_ref,
+    esend, erecv, isend, irecv, eparts, rparts, sparts, pick, ssend, srecv, tsend, trecv, values, last,
+    e_s, e_r, i_s, i_r, s_s, s_r, t_s, t_r,
+):
+    shards, groups, block, owned, width = sizes
+    shard, group = lax.axis_index("shard"), lax.axis_index("group")
+    before = lax.rem(group + groups - 1, groups)
+    edges, padded = edge_source_ref.shape[1], relation_ref.shape[0]
+    table_rows = shards * block
+    tile = 256
+    stages = ((0, block), (block, block), (2 * block, packed_rows(block) - 2 * block))
+    moves = ((0, owned), (owned, owned), (2 * owned, packed_rows(owned) - 2 * owned))
+
+    isend[...] = target_index_ref[...]
+    wide = load_wide(entity_ref, slice(None), owned, last)
+    for c in range(3):
+        esend[c * owned : (c + 1) * owned] = wide[c]
+    esend[3 * owned :] = pack_tail(wide[3])
+    greet(shards, groups, shard, group)
+
+    index_copy = remote(isend, irecv, i_s, i_r, group=before)
+    index_copy.start()
+
+    def move(stage):
+        first, size = moves[stage]
+        rows = pl.ds(first, size)
+        return remote(esend.at[rows], erecv.at[rows], e_s.at[stage], e_r.at[stage], group=before)
+
+    for stage in range(3):
+        move(stage).start()
+
+    for c in range(4):
+        for k, part in enumerate(split3(wide[c])):
+            eparts[k, :, 128 * c : 128 * c + 128] = part
+
+    def taken(parts, index_ref, t, count):
+        ones = picked(index_ref[:, pl.ds(pl.multiple_of(t * tile, tile), tile)], count)
+        return (mxu(ones, parts[0], TN) + mxu(ones, parts[1], TN)) + mxu(ones, parts[2], TN)
+
+    def take_source(t, carried):
+        value = taken(eparts, source_index_ref, t, owned)
+        for j in range(tile // block):
+            store_packed(ssend.at[t * (tile // block) + j], value[j * block : (j + 1) * block])
+        return carried
+
+    lax.fori_loop(0, table_rows // tile, take_source, 0)
+
+    def source_copy(to, slot):
+        return remote(ssend.at[to], srecv.at[slot], s_s.at[to], s_r.at[slot], shard=to)
+
+    def send_source(k, carried):
+        source_copy(lax.rem(shard + k, shards), shard).start()
+        return carried
+
+    lax.fori_loop(1, shards, send_source, 0)
+    srecv[shard] = ssend[shard]
+
+    step = 128 if padded % 128 == 0 else 32
+
+    def split_relation(t, carried):
+        rows = pl.ds(pl.multiple_of(t * step, step), step)
+        for c, x in enumerate(load_wide(relation_ref, rows, step, last)):
+            for k, part in enumerate(split3(x)):
+                rparts[k, rows, 128 * c : 128 * c + 128] = part
+        return carried
+
+    lax.fori_loop(0, padded // step, split_relation, 0)
+
+    def take_relation(t, carried):
+        rels_ref[pl.ds(pl.multiple_of(t * tile, tile), tile)] = taken(rparts, edge_relation_ref, t, padded)
+        return carried
+
+    lax.fori_loop(0, edges // tile, take_relation, 0)
+
+    index_copy.wait_recv()
+    moved_index_ref[...] = irecv[...]
+    pick[...] = picked(irecv[...], owned)
+
+    def found(chunk):
+        value = mxu(pick[...], jnp.concatenate(split3(chunk), axis=1), TN)
+        return (value[:, :128] + value[:, 128:256]) + value[:, 256:]
+
+    def target_copy(stage, to, slot):
+        first, size = stages[stage]
+        rows = pl.ds(first, size)
+        return remote(
+            tsend.at[to, rows], trecv.at[slot, rows], t_s.at[stage, to], t_r.at[stage, slot], shard=to
+        )
+
+    for stage in range(3):
+        move(stage).wait_recv()
+        chunk = erecv[stage * owned : (stage + 1) * owned]
+        tsend[:, stage * block : (stage + 1) * block] = found(chunk).reshape(shards, block, 128)
+        if stage == 2:
+            values[...] = found(unpack_tail(erecv[3 * owned :], owned))
+
+            def pack_tails(p, carried):
+                rows = pl.ds(pl.multiple_of(p * block, block), block)
+                tsend[p, 3 * block :] = pack_tail(values[rows])
+                return carried
+
+            lax.fori_loop(0, shards, pack_tails, 0)
+
+        def send_target(k, carried, stage=stage):
+            target_copy(stage, lax.rem(shard + k, shards), shard).start()
+            return carried
+
+        lax.fori_loop(1, shards, send_target, 0)
+    trecv[shard] = tsend[shard]
+
+    def wait_source(k, carried):
+        frm = lax.rem(shard + k, shards)
+        source_copy(frm, frm).wait_recv()
+        return carried
+
+    lax.fori_loop(1, shards, wait_source, 0)
+
+    def split_source(p, carried):
+        rows = pl.ds(pl.multiple_of(p * block, block), block)
+        parts, tail = load_packed(srecv.at[p], block)
+        for c, x in enumerate((*parts, tail)):
+            for k, part in enumerate(split3(x)):
+                sparts[k, rows, 128 * c : 128 * c + 128] = part
+        return carried
+
+    lax.fori_loop(0, shards, split_source, 0)
+
+    def make_queries(t, carried):
+        rows = pl.ds(pl.multiple_of(t * tile, tile), tile)
+        heads = taken(sparts, edge_source_ref, t, table_rows)
+        heads_ref[rows] = heads
+        queries_ref[rows] = product(heads, rels_ref[rows])
+        return carried
+
+    lax.fori_loop(0, edges // tile, make_queries, 0)
+
+    for stage in range(3):
+        def wait_target(k, carried, stage=stage):
+            frm = lax.rem(shard + k, shards)
+            target_copy(stage, frm, frm).wait_recv()
+            return carried
+
+        lax.fori_loop(1, shards, wait_target, 0)
+
+    def put_table(p, carried):
+        rows = pl.ds(pl.multiple_of(p * block, block), block)
+        parts, tail = load_packed(trecv.at[p], block)
+        for c, x in enumerate((*parts, tail)):
+            table_ref[rows, 128 * c : 128 * c + 128] = x
+        return carried
+
+    lax.fori_loop(0, shards, put_table, 0)
+
+    index_copy.wait_send()
+    for stage in range(3):
+        def end_target(k, carried, stage=stage):
+            target_copy(stage, lax.rem(shard + k, shards), shard).wait_send()
+            return carried
+
+        lax.fori_loop(1, shards, end_target, 0)
+        move(stage).wait_send()
+
+    def end_source(k, carried):
+        source_copy(lax.rem(shard + k, shards), shard).wait_send()
+        return carried
+
+    lax.fori_loop(1, shards, end_source, 0)
+
+
+def front_step(sizes, *operands):
+    shards, groups, block, owned, width = sizes
+    padded, edges, table_rows = operands[1].shape[0], operands[4].shape[1], shards * block
+    f32, bf16 = jnp.float32, jnp.bfloat16
+    table = pltpu.VMEM((shards, packed_rows(block), 128), f32)
+    flat = pltpu.VMEM((packed_rows(owned), 128), f32)
+    index = pltpu.VMEM((1, table_rows), jnp.int32)
+    dma = pltpu.SemaphoreType.DMA
+    return pl.pallas_call(
+        functools.partial(front_kernel, sizes),
+        in_specs=[pl.BlockSpec(memory_space=pltpu.VMEM)] * len(operands),
+        out_specs=[pl.BlockSpec(memory_space=pltpu.VMEM)] * 5,
+        out_shape=[
+            jax.ShapeDtypeStruct((table_rows, WIDE), f32),
+            jax.ShapeDtypeStruct((edges, WIDE), f32),
+            jax.ShapeDtypeStruct((edges, WIDE), f32),
+            jax.ShapeDtypeStruct((edges, WIDE), f32),
+            jax.ShapeDtypeStruct((1, table_rows), jnp.int32),
+        ],
+        scratch_shapes=[
+            flat, flat, index, index,
+            pltpu.VMEM((3, owned, WIDE), bf16),
+            pltpu.VMEM((3, padded, WIDE), bf16),
+            pltpu.VMEM((3, table_rows, WIDE), bf16),
+            pltpu.VMEM((owned, table_rows), bf16),
+            table, table, table, table,
+            pltpu.VMEM((table_rows, 128), f32),
+            pltpu.VMEM((owned, 128), f32),
+            dma((3,)), dma((3,)), dma, dma, dma((shards,)), dma((shards,)), dma((3, shards)), dma((3, shards)),
+        ],
+        compiler_params=pltpu.CompilerParams(
+            collective_id=0, has_side_effects=True, vmem_limit_bytes=60 << 20
+        ),
+        name="front_step",
+    )(*operands)
 
 
 def on_device(
@@ -748,18 +902,20 @@
     groups, shards = lax.axis_size("group"), lax.axis_size("shard")
     padded = 8 * shards * (-(-relations // (8 * shards)))
 
-    entity_wide = wide(entity)
-    moved_index = passed_along(dst_send, "group", -1)
-    moved_entity = passed_along(entity_wide, "group", -1)
-    src_rows = take_rows(entity_wide, src_send.reshape(table_rows, 1))
-    source_table = exchanged(src_rows.reshape(peers, block, WIDE), "shard").reshape(table_rows, WIDE)
-    relation_wide = jnp.pad(wide(relation), ((0, padded - relations), (0, 0)))
-    relation_state_wide = jnp.pad(relation_state[:, None], ((0, padded - relations), (0, 0)), constant_values=1.0)
-    rels = take_rows(relation_wide, edge_relation.reshape(edges, 1))
-    target_rows = take_rows(moved_entity, moved_index.reshape(table_rows, 1))
-    target_table = exchanged(target_rows.reshape(peers, block, WIDE), "shard").reshape(table_rows, WIDE)
-    heads, queries = make_queries(source_table, edge_source.reshape(edges, 1), rels)
-
+    relation_rows = jnp.pad(relation, ((0, padded - relations), (0, 0)))
+    relation_states = jnp.pad(relation_state, (0, padded - relations), constant_values=1.0).reshape(1, padded)
+    sizes = (shards, groups, block, owned, width)
+    source_index = src_send.reshape(1, table_rows)
+    edge_sources, edge_relations = edge_source.reshape(1, edges), edge_relation.reshape(1, edges)
+    target_table, heads, rels, queries, moved_index = front_step(
+        sizes,
+        entity,
+        relation_rows,
+        source_index,
+        dst_send.reshape(1, table_rows),
+        edge_sources,
+        edge_relations,
+    )
     loss, query_grad, target_grad = span_step(
         edge_count,
         edge_target.reshape(spans, 1, SPAN),
@@ -767,21 +923,22 @@
         queries,
         target_table,
     )
-    relation_part = put_rows(edge_relation.reshape(1, edges), padded, query_grad, heads)
-    source_grad = put_rows(edge_source.reshape(1, edges), table_rows, query_grad, rels)
     entity_new, relation_new = back_step(
-        (shards, groups, block, owned, width),
+        sizes,
         target_grad,
-        source_grad,
-        relation_part,
-        relation_wide,
-        relation_state_wide,
-        moved_index.reshape(1, table_rows),
-        src_send.reshape(1, table_rows),
-        entity_wide,
-        entity_state.reshape(owned, 1),
+        query_grad,
+        heads,
+        rels,
+        edge_sources,
+        edge_relations,
+        relation_rows,
+        relation_states,
+        moved_index,
+        source_index,
+        entity,
+        entity_state.reshape(1, owned),
     )
-    return narrow(entity_new, width), narrow(relation_new[:relations], width), loss.reshape(edges)
+    return entity_new, relation_new[:relations], loss.reshape(edges)
 
 
 def solution(mesh):

time: 335 us -> 270 us (0.81)
  the two profiles are of different devices: /device:TPU:57 before, /device:TPU:69 now
where the time goes in v3:
time: 270 us; the launch traced here: 264 us
  Pallas kernels  245 us (91%)
  local copies, waits for them, and re-layouts  18 us (7%)
    pallas_call x1, Pallas kernels, back_step(): pl.pallas_call(functools.partial(back_kernel, sizes), in_specs=[pl.BlockS...  165 us
    pallas_call x1, Pallas kernels, front_step(): pl.pallas_call(functools.partial(front_kernel, sizes), in_specs=[pl.Block...  57.9 us
    pallas_call x1, Pallas kernels, span_step(): pl.pallas_call(span_kernel, grid=(spans,), in_specs=[pl.BlockSpec(memory_...  22 us
    unnamed x18, local copies, waits for them, and re-layouts  12.2 us

profile of v3, /device:TPU:69, one launch (start us, length us, event | category | flops | bytes accessed | tf_op | source)
XLA Modules:
  0.0 264.5 jit_solution(10116126532407965331)
XLA Ops:
  0.6 2.5 copy.14
  3.1 0.0 copy-start.3
  3.2 0.0 copy-start.4
  3.2 1.9 pad.8.relation_ref
  5.0 2.5 copy.15.entity_ref
  7.5 0.0 copy-done.3
  7.5 0.0 copy-start.5
  7.5 0.0 copy-start.2
  7.5 0.7 reshape.35.source_index_ref
  8.2 0.0 copy-done.4
  8.2 0.7 reshape.36.target_index_ref
  8.9 57.9 %front_step.1 = (f32[1024,512]{1,0:T(8,128)}, f32[1024,512]{1,0:T(8,128)}, f32[1024,512]{1,0:T(8,128)}, f32[1024,512]{1,0:T(8,128)}, s32[1,1024]{1,0:T(1,128)}) custom-call(f32[512,400]{1,0:T(8,128)} %copy.15.entity_ref, f32[1408,400]{1,0:T(8,128)} %pad.8.relation_ref, s32[1,1024]{1,0:T(1,128)} %reshape.35.source_index_ref, ...), custom_call_target="tpu_custom_call" | custom-call | tf_op jit(solution)/shard_map/front_step/pallas_call | solution.py:853
  66.8 0.0 copy-done.5
  67.5 0.0 copy-done.2
  67.5 0.0 copy-start.6
  67.5 22.0 %span_step.1 = (f32[2,1,512]{2,1,0:T(1,128)}, f32[1024,512]{1,0:T(8,128)S(1)}, f32[1024,512]{1,0:T(8,128)S(1)}) custom-call(s32[1]{0:T(128)S(6)} %copy.19.count_ref, s32[2,1,512]{2,1,0:T(1,128)S(1)} %bitcast.5, s32[2,1,1000]{2,1,0:T(1,128)S(1)} %reshape.34.slots_ref, f32[1024,512]{1,0:T(8,128)} %get-tuple-element.13.query_ref, ...), custom_call_target="tpu_custom_call" | custom-call | flops 12884901888 | bytes 8388608 | tf_op jit(solution)/shard_map/span_step/pallas_call | solution.py:211
  89.5 1.3 copy-done
  90.8 1.3 copy-done.1
  92.1 0.0 copy-done.6
  92.1 0.6 reshape.39.relation_state_ref
  92.7 165.2 %back_step.1 = (f32[512,400]{1,0:T(8,128)}, f32[1408,400]{1,0:T(8,128)}) custom-call(f32[1024,512]{1,0:T(8,128)} %copy-done.1, f32[1024,512]{1,0:T(8,128)} %copy-done, f32[1024,512]{1,0:T(8,128)} %get-tuple-element.17.heads_ref, f32[1024,512]{1,0:T(8,128)} %get-tuple-element.18.rels_ref, s32[1,1024]{1,0:T(1,128)} %bitcast.7, s32[1,1024]{1,0:T(1,128)} %bitcast.9, ...), custom_call_target="tpu_custom_call" | custom-call | tf_op jit(solution)/shard_map/back_step/pallas_call | solution.py:648
  257.9 2.0 slice.3
  259.9 2.1 copy.18
  262.1 2.4 copy.17
  (4 shorter events, 0.0 us)
Async XLA Ops:
  3.1 4.4 %copy-start.3 = (s32[1,16,64]{2,1,0:T(8,128)S(1)}, s32[1,16,64]{2,1,0:T(8,128)}, u32[]{:S(2)}) copy-start(s32[1,16,64]{2,1,0:T(8,128)} %param.15) | copy-start | bytes 12292
  3.2 5.0 %copy-start.4 = (s32[1,16,64]{2,1,0:T(8,128)S(1)}, s32[1,16,64]{2,1,0:T(8,128)}, u32[]{:S(2)}) copy-start(s32[1,16,64]{2,1,0:T(8,128)} %param.16) | copy-start | bytes 12292
  7.5 59.3 %copy-start.5 = (s32[2,1000]{1,0:T(2,128)S(1)}, s32[2,1000]{1,0:T(2,128)}, u32[]{:S(2)}) copy-start(s32[2,1000]{1,0:T(2,128)} %param.20) | copy-start | bytes 24004
  7.5 59.9 %copy-start.2 = (s32[1024]{0:T(1024)S(1)}, s32[1024]{0:T(1024)}, u32[]{:S(2)}) copy-start(s32[1024]{0:T(1024)} %param.19) | copy-start | bytes 12292
  67.5 24.6 %copy-start.6 = (f32[1345]{0:T(1024)S(1)}, f32[1345]{0:T(1024)}, u32[]{:S(2)}) copy-start(f32[1345]{0:T(1024)} %param.14) | copy-start | bytes 16144
  89.5 1.3 copy-start
  90.8 1.3 copy-start.1

commit v4 on v3

--- a/solution.py
+++ b/solution.py
@@ -11,6 +11,7 @@
 LEARN_RATE = 0.5
 WIDE = 512
 TAIL = 8
+ACROSS = 4
 MESH = pl.DeviceIdType.MESH
 
 NT = (((1,), (1,)), ((), ()))
@@ -288,7 +289,7 @@
     )
 
 
-def greet(shards, groups, shard, group):
+def greet(shards, groups, shard, group, team=None):
     barrier = pltpu.get_barrier_semaphore()
 
     def near(k, carried):
@@ -305,7 +306,74 @@
 
     lax.fori_loop(1, shards, near, 0)
     lax.fori_loop(1, groups, far, 0)
-    pl.semaphore_wait(barrier, shards + groups - 2)
+    met = shards + groups - 2
+    if team is not None:
+        count, place, member = team
+
+        def wide_signal(k, carried):
+            pl.semaphore_signal(
+                barrier, inc=1, device_id=member(lax.rem(place + k, count)), device_id_type=MESH
+            )
+            return carried
+
+        lax.fori_loop(1, count, wide_signal, 0)
+        met = met + count - 1
+    pl.semaphore_wait(barrier, met)
+
+
+class Passing:
+    def __init__(self, groups, group, by, owned, rows_ref, via_ref, out_ref, sent, came, via_came, handed):
+        layers = groups // ACROSS
+        x, layer = lax.rem(group, ACROSS), lax.div(group, ACROSS)
+        ahead = lax.rem(layer + by + layers, layers)
+        first, last = (ACROSS - 1, 0) if by > 0 else (0, ACROSS - 1)
+        self.x, self.first, self.last = x, first, last
+        self.direct = lax.rem(group + by + groups, groups)
+        self.over = (layer * ACROSS + last, ahead * ACROSS + first)
+        self.final = (ahead * ACROSS + last, layer * ACROSS + last)
+        rest = packed_rows(owned) - 2 * owned
+        part = 8 * (rest // 16)
+        self.pieces = ((0, owned), (owned, owned), (2 * owned, part), (2 * owned + part, rest - part))
+        self.refs = (rows_ref, via_ref, out_ref)
+        self.sems = (sent, came, via_came, handed)
+
+    def copy(self, i, kind):
+        rows = pl.ds(*self.pieces[i])
+        rows_ref, via_ref, out_ref = self.refs
+        sent, came, via_came, handed = self.sems
+        if kind == "direct":
+            return remote(rows_ref.at[rows], out_ref.at[rows], sent.at[i], came.at[i], group=self.direct)
+        if kind == "over":
+            return remote(
+                rows_ref.at[rows], via_ref.at[rows], sent.at[i], via_came.at[i], group=self.over[i % 2]
+            )
+        return remote(via_ref.at[rows], out_ref.at[rows], handed.at[i], came.at[i], group=self.final[i % 2])
+
+    def send(self, i):
+        @pl.when(self.x != self.first)
+        def _():
+            self.copy(i, "direct").start()
+
+        @pl.when(self.x == self.first)
+        def _():
+            self.copy(i, "over").start()
+
+    def relay(self, i):
+        @pl.when(self.x == (self.last if i % 2 == 0 else self.first))
+        def _():
+            self.copy(i, "over").wait_recv()
+            self.copy(i, "final").start()
+
+    def wait(self, i):
+        self.copy(i, "direct").wait_recv()
+
+    def end(self):
+        for i in range(4):
+            self.copy(i, "direct").wait_send()
+
+            @pl.when(self.x == (self.last if i % 2 == 0 else self.first))
+            def _():
+                self.copy(i, "final").wait_send()
 
 
 def back_kernel(
@@ -313,22 +381,28 @@
     target_ref, query_grad_ref, heads_ref, rels_ref, edge_source_ref, edge_relation_ref,
     relation_ref, relation_state_ref, moved_index_ref, source_index_ref, entity_ref, entity_state_ref,
     entity_new_ref, relation_new_ref,
-    tsend, trecv, ssend, srecv, dense, moved, pick, values, grads, part_ref, last, dense_own,
+    tsend, trecv, ssend, srecv, dense, via, moved, pick, values, grads, part_ref, last, dense_own,
     r0send, r0recv, r1, r1recv, r2, r2recv, r3, r3recv, r4, r5,
-    t_s, t_r, s_s, s_r, p_s, p_r, r0_s, r0_r, r1_s, r1_r, r2_s, r2_r, r3_s, r3_r, r4_s, r4_r, r5_s, r5_r,
+    t_s, t_r, s_s, s_r, p_s, p_r, p_v, p_h, r0_s, r0_r, r1_s, r1_r, r2_s, r2_r, r3_s, r3_r, r4_s, r4_r, r5_s, r5_r,
 ):
     shards, groups, block, owned, width = sizes
     chips = shards // 2
     shard, group = lax.axis_index("shard"), lax.axis_index("group")
     core, chip = lax.rem(shard, 2), lax.div(shard, 2)
     partner = shard + 1 - 2 * core
-    after = lax.rem(group + 1, groups)
-    rb = part_ref.shape[0] // shards
+    across, layer = lax.rem(group, ACROSS), lax.div(group, ACROSS)
+    rb = part_ref.shape[0] // (2 * ACROSS)
+    members = r2.shape[0]
+    place = layer * chips + chip
+
+    def member(m):
+        return {"group": lax.div(m, chips) * ACROSS + across, "shard": 2 * lax.rem(m, chips) + core}
+
     piece = r2.shape[1]
     stages = ((0, block), (block, block), (2 * block, packed_rows(block) - 2 * block))
-    moves = ((0, owned), (owned, owned), (2 * owned, packed_rows(owned) - 2 * owned))
-
-    greet(shards, groups, shard, group)
+    passing = Passing(groups, group, 1, owned, dense, via, moved, p_s, p_r, p_v, p_h)
+
+    greet(shards, groups, shard, group, (members, place, member))
 
     def pack_target(p, carried):
         rows = pl.ds(pl.multiple_of(p * block, block), block)
@@ -359,7 +433,7 @@
     put_tile = half_rows // 2 if half_rows % 32 == 0 else half_rows
 
     def half_block(which, q):
-        return pl.ds(pl.multiple_of((which * chips + q) * rb, rb), rb)
+        return pl.ds(pl.multiple_of((which * ACROSS + q) * rb, rb), rb)
 
     def gradient_parts(other_ref):
         def turn(t, carried):
@@ -390,7 +464,7 @@
         store_packed(r0send.at[q], part_ref[half_block(1 - core, q)])
         return carried
 
-    lax.fori_loop(0, chips, pack_other, 0)
+    lax.fori_loop(0, ACROSS, pack_other, 0)
     pair = remote(r0send, r0recv, r0_s, r0_r, shard=partner)
     pair.start()
     half_sums(core)
@@ -399,7 +473,7 @@
         store_packed(r1.at[q], part_ref[half_block(core, q)])
         return carried
 
-    lax.fori_loop(0, chips, pack_own, 0)
+    lax.fori_loop(0, ACROSS, pack_own, 0)
     trecv[shard] = tsend[shard]
     pick[...] = picked(moved_index_ref[...], owned)
 
@@ -414,11 +488,6 @@
 
         lax.fori_loop(0, shards, turn, 0)
         return values[...]
-
-    def move(stage):
-        first, size = moves[stage]
-        rows = pl.ds(first, size)
-        return remote(dense.at[rows], moved.at[rows], p_s.at[stage], p_r.at[stage], group=after)
 
     def pass_on(stage):
         def wait_target(k, carried):
@@ -431,7 +500,9 @@
         dense[stage * owned : (stage + 1) * owned] = placed(chunk)
         if stage == 2:
             dense[3 * owned :] = pack_tail(placed(tails(trecv)))
-        move(stage).start()
+        passing.send(stage)
+        if stage == 2:
+            passing.send(3)
 
     pass_on(0)
     pair.wait_recv()
@@ -440,17 +511,20 @@
         r1[q] = r1[q] + r0recv[q]
         return carried
 
-    lax.fori_loop(0, chips, add_pair, 0)
-
-    def chip_copy(to, slot):
-        return remote(r1.at[to], r1recv.at[slot], r1_s.at[to], r1_r.at[slot], shard=2 * to + core)
-
-    def send_chip(k, carried):
-        chip_copy(lax.rem(chip + k, chips), chip).start()
-        return carried
-
-    lax.fori_loop(1, chips, send_chip, 0)
+    lax.fori_loop(0, ACROSS, add_pair, 0)
+
+    def across_copy(to, slot):
+        return remote(
+            r1.at[to], r1recv.at[slot], r1_s.at[to], r1_r.at[slot], group=layer * ACROSS + to
+        )
+
+    def send_across(k, carried):
+        across_copy(lax.rem(across + k, ACROSS), across).start()
+        return carried
+
+    lax.fori_loop(1, ACROSS, send_across, 0)
     pass_on(1)
+    passing.relay(0)
 
     gradient_parts(rels_ref)
 
@@ -471,86 +545,89 @@
 
     lax.fori_loop(1, shards, send_source, 0)
     srecv[shard] = ssend[shard]
+    passing.relay(1)
     pass_on(2)
 
     r2[...] = jnp.zeros_like(r2)
 
-    def wait_chip(k, carried):
-        frm = lax.rem(chip + k, chips)
-        chip_copy(frm, frm).wait_recv()
-        return carried
-
-    lax.fori_loop(1, chips, wait_chip, 0)
-    r1recv[chip] = r1[chip]
-    total = r1recv[0]
-    for q in range(1, chips):
-        total = total + r1recv[q]
-    size = total.shape[0]
-    for h in range(groups):
-        count = min(piece, size - h * piece)
+    def wait_across(k, carried):
+        frm = lax.rem(across + k, ACROSS)
+        across_copy(frm, frm).wait_recv()
+        return carried
+
+    lax.fori_loop(1, ACROSS, wait_across, 0)
+    r1recv[across] = r1[across]
+    total = (r1recv[0] + r1recv[1]) + (r1recv[2] + r1recv[3])
+    size, piece = total.shape[0], r2.shape[1]
+    for m in range(members):
+        count = min(piece, size - m * piece)
         if count > 0:
-            r2[h, :count] = total[h * piece : h * piece + count]
-
-    def group_copy(to, slot):
-        return remote(r2.at[to], r2recv.at[slot], r2_s.at[to], r2_r.at[slot], group=to)
-
-    def send_group(k, carried):
-        group_copy(lax.rem(group + k, groups), group).start()
-        return carried
-
-    def wait_group(k, carried):
-        frm = lax.rem(group + k, groups)
-        group_copy(frm, frm).wait_recv()
-        return carried
-
-    lax.fori_loop(1, groups, send_group, 0)
-    r2recv[group] = r2[group]
-    lax.fori_loop(1, groups, wait_group, 0)
+            r2[m, :count] = total[m * piece : m * piece + count]
+
+    def member_copy(to, slot):
+        return remote(r2.at[to], r2recv.at[slot], r2_s.at[to], r2_r.at[slot], **member(to))
+
+    def send_member(k, carried):
+        member_copy(lax.rem(place + k, members), place).start()
+        return carried
+
+    def wait_member(k, carried):
+        frm = lax.rem(place + k, members)
+        member_copy(frm, frm).wait_recv()
+        return carried
+
+    lax.fori_loop(1, members, send_member, 0)
+    passing.relay(2)
+    passing.relay(3)
+    r2recv[place] = r2[place]
+    lax.fori_loop(1, members, wait_member, 0)
     r3[...] = jnp.sum(r2recv[...], axis=0)
 
     def share_copy(to, slot):
-        return remote(r3, r3recv.at[slot], r3_s.at[to], r3_r.at[slot], group=to)
+        return remote(r3, r3recv.at[slot], r3_s.at[to], r3_r.at[slot], **member(to))
 
     def send_share(k, carried):
-        share_copy(lax.rem(group + k, groups), group).start()
+        share_copy(lax.rem(place + k, members), place).start()
         return carried
 
     def wait_share(k, carried):
-        frm = lax.rem(group + k, groups)
+        frm = lax.rem(place + k, members)
         share_copy(frm, frm).wait_recv()
         return carried
 
-    lax.fori_loop(1, groups, send_share, 0)
-    r3recv[group] = r3[...]
-    lax.fori_loop(1, groups, wait_share, 0)
+    lax.fori_loop(1, members, send_share, 0)
+    r3recv[place] = r3[...]
+    lax.fori_loop(1, members, wait_share, 0)
 
     def updated(params_, state, gradient):
         squares = sum(jnp.sum(g * g, axis=1, keepdims=True) for g in gradient)
         root = jnp.sqrt(state + squares / width)
         return [p - LEARN_RATE * g / root for p, g in zip(params_, gradient)]
 
-    summed = r3recv[...].reshape(groups * piece, 128)
+    summed = r3recv[...].reshape(members * piece, 128)
     gradient = [summed[c * rb : (c + 1) * rb] for c in range(3)]
     gradient.append(unpack_tail(summed[3 * rb : size], rb))
-    state = column_of(relation_state_ref, (core * chips + chip) * rb, rb)
-    fresh = updated(load_wide(relation_ref, half_block(core, chip), rb, last), state, gradient)
-    store_packed(r4.at[chip], jnp.concatenate(fresh, axis=1))
-
-    def spread_copy(to, slot):
-        return remote(r4.at[chip], r4.at[chip], r4_s.at[to], r4_r.at[chip], shard=2 * to + core)
+    state = column_of(relation_state_ref, (core * ACROSS + across) * rb, rb)
+    fresh = updated(load_wide(relation_ref, half_block(core, across), rb, last), state, gradient)
+    store_packed(r4.at[across], jnp.concatenate(fresh, axis=1))
+
+    def spread_copy(to):
+        return remote(
+            r4.at[across], r4.at[across], r4_s.at[to], r4_r.at[across], group=layer * ACROSS + to
+        )
 
     def spread_wait(frm):
-        return remote(r4.at[frm], r4.at[frm], r4_s.at[frm], r4_r.at[frm], shard=2 * frm + core)
+        return remote(r4.at[frm], r4.at[frm], r4_s.at[frm], r4_r.at[frm], group=layer * ACROSS + frm)
 
     def hand_copy(q):
         return remote(r4.at[q], r5.at[q], r5_s.at[q], r5_r.at[q], shard=partner)
 
     def send_spread(k, carried):
-        spread_copy(lax.rem(chip + k, chips), chip).start()
-        return carried
-
-    lax.fori_loop(1, chips, send_spread, 0)
-    hand_copy(chip).start()
+        spread_copy(lax.rem(across + k, ACROSS)).start()
+        return carried
+
+    lax.fori_loop(1, ACROSS, send_spread, 0)
+    hand_copy(across).start()
 
     def wait_source(k, carried):
         frm = lax.rem(shard + k, shards)
@@ -562,8 +639,8 @@
     for c in range(3):
         dense_own[c] = placed(srecv[:, c * block : (c + 1) * block].reshape(shards * block, 128))
     dense_own[3] = placed(tails(srecv))
-    for stage in range(3):
-        move(stage).wait_recv()
+    for i in range(4):
+        passing.wait(i)
     parts, tail = load_packed(moved, owned)
     parts.append(tail)
     gradient = [dense_own[c] + parts[c] for c in range(4)]
@@ -572,12 +649,12 @@
     store_narrow(entity_new_ref, slice(None), fresh)
 
     def forward(k, carried):
-        frm = lax.rem(chip + k, chips)
+        frm = lax.rem(across + k, ACROSS)
         spread_wait(frm).wait_recv()
         hand_copy(frm).start()
         return carried
 
-    lax.fori_loop(1, chips, forward, 0)
+    lax.fori_loop(1, ACROSS, forward, 0)
 
     def put_out(which, ref):
         def turn(q, carried):
@@ -585,7 +662,7 @@
             store_narrow(relation_new_ref, half_block(which, q), (*got, tail_))
             return carried
 
-        lax.fori_loop(0, chips, turn, 0)
+        lax.fori_loop(0, ACROSS, turn, 0)
 
     put_out(core, r4)
 
@@ -593,7 +670,7 @@
         hand_copy(q).wait_recv()
         return carried
 
-    lax.fori_loop(0, chips, take_hand, 0)
+    lax.fori_loop(0, ACROSS, take_hand, 0)
     put_out(1 - core, r5)
 
     for stage in range(3):
@@ -603,22 +680,22 @@
             return carried
 
         lax.fori_loop(1, shards, end_target, 0)
-        move(stage).wait_send()
+    passing.end()
 
     def end_shard(k, carried):
         source_copy(lax.rem(shard + k, shards), shard).wait_send()
         return carried
 
-    def end_chip(k, carried):
-        to = lax.rem(chip + k, chips)
-        chip_copy(to, chip).wait_send()
-        spread_copy(to, chip).wait_send()
-        return carried
-
-    def end_group(k, carried):
-        to = lax.rem(group + k, groups)
-        group_copy(to, group).wait_send()
-        share_copy(to, group).wait_send()
+    def end_across(k, carried):
+        to = lax.rem(across + k, ACROSS)
+        across_copy(to, across).wait_send()
+        spread_copy(to).wait_send()
+        return carried
+
+    def end_member(k, carried):
+        to = lax.rem(place + k, members)
+        member_copy(to, place).wait_send()
+        share_copy(to, place).wait_send()
         return carried
 
     def end_hand(q, carried):
@@ -626,9 +703,9 @@
         return carried
 
     lax.fori_loop(1, shards, end_shard, 0)
-    lax.fori_loop(1, chips, end_chip, 0)
-    lax.fori_loop(1, groups, end_group, 0)
-    lax.fori_loop(0, chips, end_hand, 0)
+    lax.fori_loop(1, ACROSS, end_across, 0)
+    lax.fori_loop(1, members, end_member, 0)
+    lax.fori_loop(0, ACROSS, end_hand, 0)
     pair.wait_send()
 
 
@@ -636,14 +713,14 @@
     shards, groups, block, owned, width = sizes
     padded = operands[6].shape[0]
     edges = operands[1].shape[0]
-    chips, rb = shards // 2, padded // shards
-    size = packed_rows(rb)
-    piece = 8 * (-(-size // (8 * groups)))
+    members = shards // 2 * groups // ACROSS
+    size = packed_rows(padded // (2 * ACROSS))
+    piece = 8 * (-(-size // (8 * members)))
     f32 = jnp.float32
     table = pltpu.VMEM((shards, packed_rows(block), 128), f32)
     flat = pltpu.VMEM((packed_rows(owned), 128), f32)
-    half = pltpu.VMEM((chips, size, 128), f32)
-    pieces = pltpu.VMEM((groups, piece, 128), f32)
+    half = pltpu.VMEM((ACROSS, size, 128), f32)
+    pieces = pltpu.VMEM((members, piece, 128), f32)
     dma = pltpu.SemaphoreType.DMA
     return pl.pallas_call(
         functools.partial(back_kernel, sizes),
@@ -651,7 +728,7 @@
         out_specs=[pl.BlockSpec(memory_space=pltpu.VMEM)] * 2,
         out_shape=[jax.ShapeDtypeStruct((owned, width), f32), jax.ShapeDtypeStruct((padded, width), f32)],
         scratch_shapes=[
-            table, table, table, table, flat, flat,
+            table, table, table, table, flat, flat, flat,
             pltpu.VMEM((owned, shards * block), jnp.bfloat16),
             pltpu.VMEM((shards * block, 128), f32),
             pltpu.VMEM((2, edges, WIDE), jnp.bfloat16),
@@ -659,9 +736,10 @@
             pltpu.VMEM((owned, 128), f32),
             pltpu.VMEM((4, owned, 128), f32),
             half, half, half, half, pieces, pieces, pltpu.VMEM((piece, 128), f32), pieces, half, half,
-            dma((3, shards)), dma((3, shards)), dma((shards,)), dma((shards,)), dma((3,)), dma((3,)),
-            dma, dma, dma((chips,)), dma((chips,)), dma((groups,)), dma((groups,)),
-            dma((groups,)), dma((groups,)), dma((chips,)), dma((chips,)), dma((chips,)), dma((chips,)),
+            dma((3, shards)), dma((3, shards)), dma((shards,)), dma((shards,)),
+            dma((4,)), dma((4,)), dma((4,)), dma((4,)), dma, dma, dma((ACROSS,)), dma((ACROSS,)),
+            dma((members,)), dma((members,)), dma((members,)), dma((members,)),
+            dma((ACROSS,)), dma((ACROSS,)), dma((ACROSS,)), dma((ACROSS,)),
         ],
         compiler_params=pltpu.CompilerParams(
             collective_id=1, has_side_effects=True, vmem_limit_bytes=60 << 20
@@ -674,8 +752,8 @@
     sizes,
     entity_ref, relation_ref, source_index_ref, target_index_ref, edge_source_ref, edge_relation_ref,
     table_ref, heads_ref, rels_ref, queries_ref, moved_index_ref,
-    esend, erecv, isend, irecv, eparts, rparts, sparts, pick, ssend, srecv, tsend, trecv, values, last,
-    e_s, e_r, i_s, i_r, s_s, s_r, t_s, t_r,
+    esend, evia, erecv, isend, irecv, eparts, rparts, sparts, pick, ssend, srecv, tsend, trecv, values, last,
+    e_s, e_r, e_v, e_h, i_s, i_r, s_s, s_r, t_s, t_r,
 ):
     shards, groups, block, owned, width = sizes
     shard, group = lax.axis_index("shard"), lax.axis_index("group")
@@ -684,7 +762,6 @@
     table_rows = shards * block
     tile = 256
     stages = ((0, block), (block, block), (2 * block, packed_rows(block) - 2 * block))
-    moves = ((0, owned), (owned, owned), (2 * owned, packed_rows(owned) - 2 * owned))
 
     isend[...] = target_index_ref[...]
     wide = load_wide(entity_ref, slice(None), owned, last)
@@ -696,13 +773,9 @@
     index_copy = remote(isend, irecv, i_s, i_r, group=before)
     index_copy.start()
 
-    def move(stage):
-        first, size = moves[stage]
-        rows = pl.ds(first, size)
-        return remote(esend.at[rows], erecv.at[rows], e_s.at[stage], e_r.at[stage], group=before)
-
-    for stage in range(3):
-        move(stage).start()
+    passing = Passing(groups, group, -1, owned, esend, evia, erecv, e_s, e_r, e_v, e_h)
+    for i in range(4):
+        passing.send(i)
 
     for c in range(4):
         for k, part in enumerate(split3(wide[c])):
@@ -729,6 +802,8 @@
 
     lax.fori_loop(1, shards, send_source, 0)
     srecv[shard] = ssend[shard]
+    passing.relay(0)
+    passing.relay(1)
 
     step = 128 if padded % 128 == 0 else 32
 
@@ -740,6 +815,8 @@
         return carried
 
     lax.fori_loop(0, padded // step, split_relation, 0)
+    passing.relay(2)
+    passing.relay(3)
 
     def take_relation(t, carried):
         rels_ref[pl.ds(pl.multiple_of(t * tile, tile), tile)] = taken(rparts, edge_relation_ref, t, padded)
@@ -763,7 +840,9 @@
         )
 
     for stage in range(3):
-        move(stage).wait_recv()
+        passing.wait(stage)
+        if stage == 2:
+            passing.wait(3)
         chunk = erecv[stage * owned : (stage + 1) * owned]
         tsend[:, stage * block : (stage + 1) * block] = found(chunk).reshape(shards, block, 128)
         if stage == 2:
@@ -833,7 +912,7 @@
             return carried
 
         lax.fori_loop(1, shards, end_target, 0)
-        move(stage).wait_send()
+    passing.end()
 
     def end_source(k, carried):
         source_copy(lax.rem(shard + k, shards), shard).wait_send()
@@ -862,7 +941,7 @@
             jax.ShapeDtypeStruct((1, table_rows), jnp.int32),
         ],
         scratch_shapes=[
-            flat, flat, index, index,
+            flat, flat, flat, index, index,
             pltpu.VMEM((3, owned, WIDE), bf16),
             pltpu.VMEM((3, padded, WIDE), bf16),
             pltpu.VMEM((3, table_rows, WIDE), bf16),
@@ -870,7 +949,8 @@
             table, table, table, table,
             pltpu.VMEM((table_rows, 128), f32),
             pltpu.VMEM((owned, 128), f32),
-            dma((3,)), dma((3,)), dma, dma, dma((shards,)), dma((shards,)), dma((3, shards)), dma((3, shards)),
+            dma((4,)), dma((4,)), dma((4,)), dma((4,)), dma, dma,
+            dma((shards,)), dma((shards,)), dma((3, shards)), dma((3, shards)),
         ],
         compiler_params=pltpu.CompilerParams(
             collective_id=0, has_side_effects=True, vmem_limit_bytes=60 << 20
@@ -900,7 +980,8 @@
     edges = edge_source.shape[0]
     spans = edges // SPAN
     groups, shards = lax.axis_size("group"), lax.axis_size("shard")
-    padded = 8 * shards * (-(-relations // (8 * shards)))
+    unit = max(8 * shards, 16 * ACROSS)
+    padded = unit * (-(-relations // unit))
 
     relation_rows = jnp.pad(relation, ((0, padded - relations), (0, 0)))
     relation_states = jnp.pad(relation_state, (0, padded - relations), constant_values=1.0).reshape(1, padded)

time: 270 us -> 235 us (0.87); the launches traced: 264 us -> 235 us
  Pallas kernels: 245 us -> 215 us
    pallas_call x1, Pallas kernels: 165 us -> 135 us  [back_step(): pl.pallas_call(functools.partial(back_kernel, sizes), in_specs=[pl.BlockS...]
where the time goes in v4:
time: 235 us
  Pallas kernels  215 us (91%)
  local copies, waits for them, and re-layouts  18 us (8%)
    pallas_call x1, Pallas kernels, back_step(): pl.pallas_call(functools.partial(back_kernel, sizes), in_specs=[pl.BlockS...  135 us
    pallas_call x1, Pallas kernels, front_step(): pl.pallas_call(functools.partial(front_kernel, sizes), in_specs=[pl.Block...  58 us
    pallas_call x1, Pallas kernels, span_step(): pl.pallas_call(span_kernel, grid=(spans,), in_specs=[pl.BlockSpec(memory_...  22 us
    unnamed x18, local copies, waits for them, and re-layouts  12.2 us

profile of v4, /device:TPU:69, one launch (start us, length us, event | category | flops | bytes accessed | tf_op | source)
XLA Modules:
  0.0 234.9 jit_solution(1041917617427091422)
XLA Ops:
  0.6 2.5 %copy.14 = f32[1345,400]{1,0:T(8,128)S(1)} copy(f32[1345,400]{0,1:T(8,128)} %param.13) | data formatting | bytes 4304000 | tf_op args[2]
  3.1 0.0 copy-start.3
  3.2 0.0 copy-start.4
  3.2 1.9 pad.8.relation_ref
  5.0 2.5 %copy.15.entity_ref = f32[512,400]{1,0:T(8,128)} copy(f32[512,400]{0,1:T(8,128)} %param.11) | data formatting | bytes 1638400 | tf_op args[0]
  7.5 0.0 copy-done.3
  7.5 0.0 copy-start.5
  7.5 0.0 copy-start.2
  7.5 0.7 reshape.35.source_index_ref
  8.2 0.0 copy-done.4
  8.2 0.7 reshape.36.target_index_ref
  8.9 58.0 %front_step.1 = (f32[1024,512]{1,0:T(8,128)}, f32[1024,512]{1,0:T(8,128)}, f32[1024,512]{1,0:T(8,128)}, f32[1024,512]{1,0:T(8,128)}, s32[1,1024]{1,0:T(1,128)}) custom-call(f32[512,400]{1,0:T(8,128)} %copy.15.entity_ref, f32[1408,400]{1,0:T(8,128)} %pad.8.relation_ref, s32[1,1024]{1,0:T(1,128)} %reshape.35.source_index_ref, ...), custom_call_target="tpu_custom_call" | custom-call | tf_op jit(solution)/shard_map/front_step/pallas_call | solution.py:932
  66.9 0.0 copy-done.5
  67.6 0.0 copy-done.2
  67.6 0.0 copy-start.6
  67.6 22.0 %span_step.1 = (f32[2,1,512]{2,1,0:T(1,128)}, f32[1024,512]{1,0:T(8,128)S(1)}, f32[1024,512]{1,0:T(8,128)S(1)}) custom-call(s32[1]{0:T(128)S(6)} %copy.19.count_ref, s32[2,1,512]{2,1,0:T(1,128)S(1)} %bitcast.5, s32[2,1,1000]{2,1,0:T(1,128)S(1)} %reshape.34.slots_ref, f32[1024,512]{1,0:T(8,128)} %get-tuple-element.13.query_ref, ...), custom_call_target="tpu_custom_call" | custom-call | flops 12884901888 | bytes 8388608 | tf_op jit(solution)/shard_map/span_step/pallas_call | solution.py:212
  89.6 1.3 copy-done
  90.9 1.3 copy-done.1
  92.2 0.0 copy-done.6
  92.3 0.6 reshape.39.relation_state_ref
  92.9 135.4 %back_step.1 = (f32[512,400]{1,0:T(8,128)}, f32[1408,400]{1,0:T(8,128)}) custom-call(f32[1024,512]{1,0:T(8,128)} %copy-done.1, f32[1024,512]{1,0:T(8,128)} %copy-done, f32[1024,512]{1,0:T(8,128)} %get-tuple-element.17.heads_ref, f32[1024,512]{1,0:T(8,128)} %get-tuple-element.18.rels_ref, s32[1,1024]{1,0:T(1,128)} %bitcast.7, s32[1,1024]{1,0:T(1,128)} %bitcast.9, ...), custom_call_target="tpu_custom_call" | custom-call | tf_op jit(solution)/shard_map/back_step/pallas_call | solution.py:725
  228.3 2.0 slice.3
  230.3 2.1 copy.18
  232.4 2.4 %copy.17 = f32[512,400]{0,1:T(8,128)} copy(f32[512,400]{1,0:T(8,128)} %get-tuple-element.23) | data formatting | bytes 1638400
  (4 shorter events, 0.0 us)
Async XLA Ops:
  3.1 4.4 %copy-start.3 = (s32[1,16,64]{2,1,0:T(8,128)S(1)}, s32[1,16,64]{2,1,0:T(8,128)}, u32[]{:S(2)}) copy-start(s32[1,16,64]{2,1,0:T(8,128)} %param.15) | copy-start | bytes 12292
  3.2 5.0 %copy-start.4 = (s32[1,16,64]{2,1,0:T(8,128)S(1)}, s32[1,16,64]{2,1,0:T(8,128)}, u32[]{:S(2)}) copy-start(s32[1,16,64]{2,1,0:T(8,128)} %param.16) | copy-start | bytes 12292
  7.5 59.4 %copy-start.5 = (s32[2,1000]{1,0:T(2,128)S(1)}, s32[2,1000]{1,0:T(2,128)}, u32[]{:S(2)}) copy-start(s32[2,1000]{1,0:T(2,128)} %param.20) | copy-start | bytes 24004
  7.5 60.1 %copy-start.2 = (s32[1024]{0:T(1024)S(1)}, s32[1024]{0:T(1024)}, u32[]{:S(2)}) copy-start(s32[1024]{0:T(1024)} %param.19) | copy-start | bytes 12292
  67.6 24.6 %copy-start.6 = (f32[1345]{0:T(1024)S(1)}, f32[1345]{0:T(1024)}, u32[]{:S(2)}) copy-start(f32[1345]{0:T(1024)} %param.14) | copy-start | bytes 16144
  89.6 1.3 copy-start
  90.9 1.3 copy-start.1

commit v5 on v4

--- a/solution.py
+++ b/solution.py
@@ -122,36 +122,24 @@
     return jnp.where(rows == index, 1.0, 0.0).astype(jnp.bfloat16)
 
 
-def vmem(shape, index_map):
-    return pl.BlockSpec(shape, index_map, memory_space=pltpu.VMEM)
-
-
-def params(limit=48 << 20):
-    return pltpu.CompilerParams(vmem_limit_bytes=limit)
-
-
-def span_kernel(
-    count_ref, target_ref, slots_ref, query_ref, table_ref,
+def span_part(
+    span, count_ref, target_ref, slots_ref, query_ref, table_ref,
     loss_ref, query_grad_ref, target_grad_ref,
     score_ref, times_ref, parts_ref, query_parts_ref,
 ):
-    span = pl.program_id(0)
     table_rows = table_ref.shape[0]
     tile = min(256, table_rows)
     tiles = table_rows // tile
 
-    @pl.when(span == 0)
-    def _():
-        for k, part in enumerate(split3(table_ref[...])):
-            parts_ref[k] = part
-
-    for k, part in enumerate(split3(query_ref[...])):
+    edges_here = pl.ds(pl.multiple_of(span * SPAN, SPAN), SPAN)
+
+    for k, part in enumerate(split3(query_ref[edges_here])):
         query_parts_ref[k] = part
 
     edge = lax.broadcasted_iota(jnp.int32, (1, SPAN), 1) + span * SPAN
     live = jnp.where(edge < count_ref[0], 1.0, 0.0)
-    target = target_ref[0]
-    slots = slots_ref[0]
+    target = target_ref[span]
+    slots = slots_ref[span]
 
     def score_turn(t, carried):
         peak, pos = carried
@@ -182,14 +170,10 @@
 
     total = lax.fori_loop(0, tiles, total_turn, jnp.exp(pos - peak))
     log_total = peak + jnp.log(total)
-    loss_ref[0] = (log_total - pos) * live
+    loss_ref[span] = (log_total - pos) * live
     pos_grad = (jnp.exp(pos - log_total) - 1.0) * live
     scale = jnp.exp(peak - log_total) * live
-    query_grad_ref[...] = jnp.zeros_like(query_grad_ref)
-
-    @pl.when(span == 0)
-    def _():
-        target_grad_ref[...] = jnp.zeros_like(target_grad_ref)
+    query_grad_ref[edges_here] = jnp.zeros((SPAN, WIDE), jnp.float32)
 
     def grad_turn(t, carried):
         rows = pl.ds(pl.multiple_of(t * tile, tile), tile)
@@ -198,51 +182,11 @@
         w0, w1 = split2(weight)
         t0, t1 = parts_ref[0, rows], parts_ref[1, rows]
         q0, q1 = query_parts_ref[0], query_parts_ref[1]
-        query_grad_ref[...] += (mxu(w0, t1, TN) + mxu(w1, t0, TN)) + mxu(w0, t0, TN)
+        query_grad_ref[edges_here] += (mxu(w0, t1, TN) + mxu(w1, t0, TN)) + mxu(w0, t0, TN)
         target_grad_ref[rows] += (mxu(w0, q1, NN) + mxu(w1, q0, NN)) + mxu(w0, q0, NN)
         return carried
 
     lax.fori_loop(0, tiles, grad_turn, 0)
-
-
-def span_step(edge_count, target, slots, queries, table):
-    spans, negatives = slots.shape[0], slots.shape[2]
-    table_rows = table.shape[0]
-    f32 = jnp.float32
-    return pl.pallas_call(
-        span_kernel,
-        grid=(spans,),
-        in_specs=[
-            pl.BlockSpec(memory_space=pltpu.SMEM),
-            vmem((1, 1, SPAN), lambda i: (i, 0, 0)),
-            vmem((1, 1, negatives), lambda i: (i, 0, 0)),
-            vmem((SPAN, WIDE), lambda i: (i, 0)),
-            vmem((table_rows, WIDE), lambda i: (0, 0)),
-        ],
-        out_specs=[
-            vmem((1, 1, SPAN), lambda i: (i, 0, 0)),
-            vmem((SPAN, WIDE), lambda i: (i, 0)),
-            vmem((table_rows, WIDE), lambda i: (0, 0)),
-        ],
-        out_shape=[
-            jax.ShapeDtypeStruct((spans, 1, SPAN), f32),
-            jax.ShapeDtypeStruct((spans * SPAN, WIDE), f32),
-            jax.ShapeDtypeStruct((table_rows, WIDE), f32),
-        ],
-        scratch_shapes=[
-            pltpu.VMEM((table_rows, SPAN), f32),
-            pltpu.VMEM((table_rows, 1), f32),
-            pltpu.VMEM((3, table_rows, WIDE), jnp.bfloat16),
-            pltpu.VMEM((3, SPAN, WIDE), jnp.bfloat16),
-        ],
-        compiler_params=params(),
-        cost_estimate=pl.CostEstimate(
-            flops=24 * spans * SPAN * table_rows * WIDE,
-            bytes_accessed=16 * table_rows * WIDE,
-            transcendentals=spans * SPAN * table_rows,
-        ),
-        name="span_step",
-    )(edge_count, target, slots, queries, table)
 
 
 def pack_tail(x):
@@ -376,8 +320,8 @@
                 self.copy(i, "final").wait_send()
 
 
-def back_kernel(
-    sizes,
+def back_part(
+    sizes, team,
     target_ref, query_grad_ref, heads_ref, rels_ref, edge_source_ref, edge_relation_ref,
     relation_ref, relation_state_ref, moved_index_ref, source_index_ref, entity_ref, entity_state_ref,
     entity_new_ref, relation_new_ref,
@@ -390,19 +334,12 @@
     shard, group = lax.axis_index("shard"), lax.axis_index("group")
     core, chip = lax.rem(shard, 2), lax.div(shard, 2)
     partner = shard + 1 - 2 * core
+    rb = relation_ref.shape[0] // (2 * ACROSS)
+    members = r2.shape[0]
     across, layer = lax.rem(group, ACROSS), lax.div(group, ACROSS)
-    rb = part_ref.shape[0] // (2 * ACROSS)
-    members = r2.shape[0]
-    place = layer * chips + chip
-
-    def member(m):
-        return {"group": lax.div(m, chips) * ACROSS + across, "shard": 2 * lax.rem(m, chips) + core}
-
-    piece = r2.shape[1]
+    _, place, member = team
     stages = ((0, block), (block, block), (2 * block, packed_rows(block) - 2 * block))
     passing = Passing(groups, group, 1, owned, dense, via, moved, p_s, p_r, p_v, p_h)
-
-    greet(shards, groups, shard, group, (members, place, member))
 
     def pack_target(p, carried):
         rows = pl.ds(pl.multiple_of(p * block, block), block)
@@ -427,7 +364,7 @@
         lax.fori_loop(1, shards, send_target, 0)
 
     edges = query_grad_ref.shape[0]
-    padded = part_ref.shape[0]
+    padded = relation_ref.shape[0]
     tile = 256
     half_rows = padded // 2
     put_tile = half_rows // 2 if half_rows % 32 == 0 else half_rows
@@ -447,7 +384,7 @@
     def summed_rows(index_ref, first, count):
         number = lax.broadcasted_iota(jnp.int32, (count, edges), 0) + first
         ones = jnp.where(number == index_ref[...], 1.0, 0.0).astype(jnp.bfloat16)
-        return mxu(ones, grads[1], NN) + mxu(ones, grads[0], NN)
+        return mxu(ones, grads[1, :edges], NN) + mxu(ones, grads[0, :edges], NN)
 
     def half_sums(which):
         def turn(t, carried):
@@ -709,47 +646,8 @@
     pair.wait_send()
 
 
-def back_step(sizes, *operands):
-    shards, groups, block, owned, width = sizes
-    padded = operands[6].shape[0]
-    edges = operands[1].shape[0]
-    members = shards // 2 * groups // ACROSS
-    size = packed_rows(padded // (2 * ACROSS))
-    piece = 8 * (-(-size // (8 * members)))
-    f32 = jnp.float32
-    table = pltpu.VMEM((shards, packed_rows(block), 128), f32)
-    flat = pltpu.VMEM((packed_rows(owned), 128), f32)
-    half = pltpu.VMEM((ACROSS, size, 128), f32)
-    pieces = pltpu.VMEM((members, piece, 128), f32)
-    dma = pltpu.SemaphoreType.DMA
-    return pl.pallas_call(
-        functools.partial(back_kernel, sizes),
-        in_specs=[pl.BlockSpec(memory_space=pltpu.VMEM)] * len(operands),
-        out_specs=[pl.BlockSpec(memory_space=pltpu.VMEM)] * 2,
-        out_shape=[jax.ShapeDtypeStruct((owned, width), f32), jax.ShapeDtypeStruct((padded, width), f32)],
-        scratch_shapes=[
-            table, table, table, table, flat, flat, flat,
-            pltpu.VMEM((owned, shards * block), jnp.bfloat16),
-            pltpu.VMEM((shards * block, 128), f32),
-            pltpu.VMEM((2, edges, WIDE), jnp.bfloat16),
-            pltpu.VMEM((padded, WIDE), f32),
-            pltpu.VMEM((owned, 128), f32),
-            pltpu.VMEM((4, owned, 128), f32),
-            half, half, half, half, pieces, pieces, pltpu.VMEM((piece, 128), f32), pieces, half, half,
-            dma((3, shards)), dma((3, shards)), dma((shards,)), dma((shards,)),
-            dma((4,)), dma((4,)), dma((4,)), dma((4,)), dma, dma, dma((ACROSS,)), dma((ACROSS,)),
-            dma((members,)), dma((members,)), dma((members,)), dma((members,)),
-            dma((ACROSS,)), dma((ACROSS,)), dma((ACROSS,)), dma((ACROSS,)),
-        ],
-        compiler_params=pltpu.CompilerParams(
-            collective_id=1, has_side_effects=True, vmem_limit_bytes=60 << 20
-        ),
-        name="back_step",
-    )(*operands)
-
-
-def front_kernel(
-    sizes,
+def front_part(
+    sizes, team,
     entity_ref, relation_ref, source_index_ref, target_index_ref, edge_source_ref, edge_relation_ref,
     table_ref, heads_ref, rels_ref, queries_ref, moved_index_ref,
     esend, evia, erecv, isend, irecv, eparts, rparts, sparts, pick, ssend, srecv, tsend, trecv, values, last,
@@ -768,7 +666,7 @@
     for c in range(3):
         esend[c * owned : (c + 1) * owned] = wide[c]
     esend[3 * owned :] = pack_tail(wide[3])
-    greet(shards, groups, shard, group)
+    greet(shards, groups, shard, group, team)
 
     index_copy = remote(isend, irecv, i_s, i_r, group=before)
     index_copy.start()
@@ -783,7 +681,8 @@
 
     def taken(parts, index_ref, t, count):
         ones = picked(index_ref[:, pl.ds(pl.multiple_of(t * tile, tile), tile)], count)
-        return (mxu(ones, parts[0], TN) + mxu(ones, parts[1], TN)) + mxu(ones, parts[2], TN)
+        p0, p1, p2 = (parts[k, :count] for k in range(3))
+        return (mxu(ones, p0, TN) + mxu(ones, p1, TN)) + mxu(ones, p2, TN)
 
     def take_source(t, carried):
         value = taken(eparts, source_index_ref, t, owned)
@@ -921,41 +820,122 @@
     lax.fori_loop(1, shards, end_source, 0)
 
 
-def front_step(sizes, *operands):
+def step_kernel(
+    sizes,
+    count_ref, entity_ref, entity_state_ref, relation_ref, relation_state_ref,
+    source_index_ref, target_index_ref, edge_source_ref, edge_relation_ref, edge_target_ref, slots_ref,
+    entity_new_ref, relation_new_ref, loss_ref,
+    table, heads, rels, queries, query_grad, target_grad, moved_index,
+    esend, evia, erecv, isend, irecv, eparts, rparts, tparts, query_parts, pick, ssend, srecv, tsend, trecv,
+    values, last, part, times,
+    trecv_back, srecv_back, via_back, moved, own,
+    r0send, r0recv, r1, r1recv, r2, r2recv, r3, r3recv, r4, r5,
+    *sems,
+):
     shards, groups, block, owned, width = sizes
-    padded, edges, table_rows = operands[1].shape[0], operands[4].shape[1], shards * block
+    chips = shards // 2
+    shard, group = lax.axis_index("shard"), lax.axis_index("group")
+    core, chip = lax.rem(shard, 2), lax.div(shard, 2)
+    across, layer = lax.rem(group, ACROSS), lax.div(group, ACROSS)
+
+    def member(m):
+        return {"group": lax.div(m, chips) * ACROSS + across, "shard": 2 * lax.rem(m, chips) + core}
+
+    team = (r2.shape[0], layer * chips + chip, member)
+    front_part(
+        sizes, team,
+        entity_ref, relation_ref, source_index_ref, target_index_ref, edge_source_ref, edge_relation_ref,
+        table, heads, rels, queries, moved_index,
+        esend, evia, erecv, isend, irecv, eparts, rparts, tparts, pick, ssend, srecv, tsend, trecv,
+        values, last,
+        *sems[:10],
+    )
+
+    target_grad[...] = jnp.zeros_like(target_grad)
+    table_rows = table.shape[0]
+    tile = min(256, table_rows)
+
+    def split_table(t, carried):
+        rows = pl.ds(pl.multiple_of(t * tile, tile), tile)
+        for k, piece in enumerate(split3(table[rows])):
+            tparts[k, rows] = piece
+        return carried
+
+    lax.fori_loop(0, table_rows // tile, split_table, 0)
+
+    def span_turn(span, carried):
+        span_part(
+            span, count_ref, edge_target_ref, slots_ref, queries, table,
+            loss_ref, query_grad, target_grad, part, times, tparts, query_parts,
+        )
+        return carried
+
+    lax.fori_loop(0, loss_ref.shape[0], span_turn, 0)
+
+    back_part(
+        sizes, team,
+        target_grad, query_grad, heads, rels, edge_source_ref, edge_relation_ref,
+        relation_ref, relation_state_ref, moved_index, source_index_ref, entity_ref, entity_state_ref,
+        entity_new_ref, relation_new_ref,
+        tsend, trecv_back, ssend, srecv_back, esend, via_back, moved, pick, values, rparts, part, last, own,
+        r0send, r0recv, r1, r1recv, r2, r2recv, r3, r3recv, r4, r5,
+        *sems[10:],
+    )
+
+
+def whole_step(sizes, *operands):
+    shards, groups, block, owned, width = sizes
+    relation, edge_target = operands[3], operands[9]
+    padded, spans = relation.shape[0], edge_target.shape[0]
+    edges, table_rows = spans * SPAN, shards * block
+    members = shards // 2 * groups // ACROSS
+    size = packed_rows(padded // (2 * ACROSS))
+    piece = 8 * (-(-size // (8 * members)))
     f32, bf16 = jnp.float32, jnp.bfloat16
-    table = pltpu.VMEM((shards, packed_rows(block), 128), f32)
+    blocks = pltpu.VMEM((shards, packed_rows(block), 128), f32)
     flat = pltpu.VMEM((packed_rows(owned), 128), f32)
     index = pltpu.VMEM((1, table_rows), jnp.int32)
-    dma = pltpu.SemaphoreType.DMA
+    of_edges, of_table = pltpu.VMEM((edges, WIDE), f32), pltpu.VMEM((table_rows, WIDE), f32)
+    half = pltpu.VMEM((ACROSS, size, 128), f32)
+    pieces = pltpu.VMEM((members, piece, 128), f32)
+
+    def dma(*shape):
+        return [pltpu.SemaphoreType.DMA(shape), pltpu.SemaphoreType.DMA(shape)]
+
+    in_vmem = pl.BlockSpec(memory_space=pltpu.VMEM)
     return pl.pallas_call(
-        functools.partial(front_kernel, sizes),
-        in_specs=[pl.BlockSpec(memory_space=pltpu.VMEM)] * len(operands),
-        out_specs=[pl.BlockSpec(memory_space=pltpu.VMEM)] * 5,
+        functools.partial(step_kernel, sizes),
+        in_specs=[pl.BlockSpec(memory_space=pltpu.SMEM)] + [in_vmem] * (len(operands) - 1),
+        out_specs=[in_vmem] * 3,
         out_shape=[
-            jax.ShapeDtypeStruct((table_rows, WIDE), f32),
-            jax.ShapeDtypeStruct((edges, WIDE), f32),
-            jax.ShapeDtypeStruct((edges, WIDE), f32),
-            jax.ShapeDtypeStruct((edges, WIDE), f32),
-            jax.ShapeDtypeStruct((1, table_rows), jnp.int32),
+            jax.ShapeDtypeStruct((owned, width), f32),
+            jax.ShapeDtypeStruct((padded, width), f32),
+            jax.ShapeDtypeStruct((spans, 1, SPAN), f32),
         ],
         scratch_shapes=[
+            of_table, of_edges, of_edges, of_edges, of_edges, of_table, index,
             flat, flat, flat, index, index,
             pltpu.VMEM((3, owned, WIDE), bf16),
-            pltpu.VMEM((3, padded, WIDE), bf16),
+            pltpu.VMEM((3, max(padded, edges), WIDE), bf16),
             pltpu.VMEM((3, table_rows, WIDE), bf16),
+            pltpu.VMEM((3, SPAN, WIDE), bf16),
             pltpu.VMEM((owned, table_rows), bf16),
-            table, table, table, table,
+            blocks, blocks, blocks, blocks,
             pltpu.VMEM((table_rows, 128), f32),
             pltpu.VMEM((owned, 128), f32),
-            dma((4,)), dma((4,)), dma((4,)), dma((4,)), dma, dma,
-            dma((shards,)), dma((shards,)), dma((3, shards)), dma((3, shards)),
+            pltpu.VMEM((max(padded, table_rows), WIDE), f32),
+            pltpu.VMEM((table_rows, 1), f32),
+            blocks, blocks, flat, flat,
+            pltpu.VMEM((4, owned, 128), f32),
+            half, half, half, half, pieces, pieces, pltpu.VMEM((piece, 128), f32), pieces, half, half,
+            *dma(4), *dma(4), *dma(), *dma(shards), *dma(3, shards),
+            *dma(3, shards), *dma(shards), *dma(4), *dma(4), *dma(), *dma(ACROSS),
+            *dma(members), *dma(members), *dma(ACROSS), *dma(ACROSS),
         ],
         compiler_params=pltpu.CompilerParams(
-            collective_id=0, has_side_effects=True, vmem_limit_bytes=60 << 20
+            collective_id=0, has_side_effects=True, vmem_limit_bytes=67043328
         ),
-        name="front_step",
+        name="whole_step",
     )(*operands)
 
 
@@ -988,36 +968,19 @@
     sizes = (shards, groups, block, owned, width)
     source_index = src_send.reshape(1, table_rows)
     edge_sources, edge_relations = edge_source.reshape(1, edges), edge_relation.reshape(1, edges)
-    target_table, heads, rels, queries, moved_index = front_step(
+    entity_new, relation_new, loss = whole_step(
         sizes,
+        edge_count,
         entity,
+        entity_state.reshape(1, owned),
         relation_rows,
+        relation_states,
         source_index,
         dst_send.reshape(1, table_rows),
         edge_sources,
         edge_relations,
-    )
-    loss, query_grad, target_grad = span_step(
-        edge_count,
         edge_target.reshape(spans, 1, SPAN),
         neg_slots.reshape(spans, 1, neg_slots.shape[1]),
-        queries,
-        target_table,
-    )
-    entity_new, relation_new = back_step(
-        sizes,
-        target_grad,
-        query_grad,
-        heads,
-        rels,
-        edge_sources,
-        edge_relations,
-        relation_rows,
-        relation_states,
-        moved_index,
-        source_index,
-        entity,
-        entity_state.reshape(1, owned),
     )
     return entity_new, relation_new[:relations], loss.reshape(edges)
 

time: 235 us -> 224 us (0.953)
  Pallas kernels: 215 us -> 203 us
    pallas_call x3 -> x1, Pallas kernels: 215 us -> 203 us  [whole_step(): pl.pallas_call(functools.partial(step_kernel, sizes), in_specs=[pl.BlockS...]
    unnamed x18 -> x7, local copies, waits for them, and re-layouts: 12.2 us -> 10.1 us
where the time goes in v5:
time: 224 us; the launch traced here: 223 us
  Pallas kernels  203 us (91%)
  local copies, waits for them, and re-layouts  19.3 us (9%)
    pallas_call x1, Pallas kernels, whole_step(): pl.pallas_call(functools.partial(step_kernel, sizes), in_specs=[pl.BlockS...  203 us
    unnamed x7, local copies, waits for them, and re-layouts  10.1 us

profile of v5, /device:TPU:69, one launch (start us, length us, event | category | flops | bytes accessed | tf_op | source)
XLA Modules:
  0.0 223.2 jit_solution(14864369048961827145)
XLA Ops:
  1.3 1.4 reshape.35.source_index_ref
  2.6 1.4 reshape.36.target_index_ref
  4.0 0.7 pad.9
  4.7 0.6 reshape.34.relation_state_ref
  5.3 1.3 reshape.40.slots_ref
  6.6 2.5 %copy.15.entity_ref = f32[512,400]{1,0:T(8,128)} copy(f32[512,400]{0,1:T(8,128)} %param.11) | data formatting | bytes 1638400 | tf_op args[0]
  9.1 2.5 %copy.14 = f32[1345,400]{1,0:T(8,128)S(1)} copy(f32[1345,400]{0,1:T(8,128)} %param.13) | data formatting | bytes 4304000 | tf_op args[2]
  11.6 1.9 pad.8.relation_ref
  13.4 202.6 %whole_step.1 = (f32[512,400]{1,0:T(8,128)}, f32[1408,400]{1,0:T(8,128)}, f32[2,1,512]{2,1,0:T(1,128)}) custom-call(s32[1]{0:T(128)S(6)} %copy.19.count_ref, f32[512,400]{1,0:T(8,128)} %copy.15.entity_ref, f32[1,512]{1,0:T(1,128)} %bitcast.9, f32[1408,400]{1,0:T(8,128)} %pad.8.relation_ref, f32[1,1408]{1,0:T(1,128)} %reshape.34.relation_state_ref, ...), custom_call_target="tpu_custom_call" | custom-call | tf_op jit(solution)/shard_map/whole_step/pallas_call | solution.py:906
  216.0 2.4 %copy.16 = f32[512,400]{0,1:T(8,128)} copy(f32[512,400]{1,0:T(8,128)} %get-tuple-element.9) | data formatting | bytes 1638400
  218.4 2.0 slice.3
  220.5 0.0 copy-start
  220.5 2.1 copy.17
  222.6 0.0 copy-done
  222.6 0.6 copy.20
Async XLA Ops:
  220.5 2.1 copy-start

commit v6 on v5

--- a/solution.py
+++ b/solution.py
@@ -70,6 +70,21 @@
     for c in range(3):
         ref[rows, 128 * c : 128 * c + 128] = x[c]
     ref[rows, 384:400] = x[3][:, :16]
+
+
+def load_turned(ref):
+    n = ref.shape[1]
+    both = jnp.concatenate([ref[128:192], ref[328:392]], axis=0)
+    tail = jnp.concatenate([ref[192:200], ref[392:400], jnp.zeros((112, n), jnp.float32)], axis=0)
+    return ref[0:128].T, ref[200:328].T, both.T, tail.T
+
+
+def store_turned(ref, parts):
+    real, imag, both, tail = (x.T for x in parts)
+    ref[0:128] = real
+    ref[200:328] = imag
+    ref[128:192], ref[328:392] = both[:64], both[64:]
+    ref[192:200], ref[392:400] = tail[:8], tail[8:16]
 
 
 def column_of(row_ref, first, count):
@@ -133,21 +148,20 @@
 
     edges_here = pl.ds(pl.multiple_of(span * SPAN, SPAN), SPAN)
 
-    for k, part in enumerate(split3(query_ref[edges_here])):
+    for k, part in enumerate(split2(query_ref[edges_here])):
         query_parts_ref[k] = part
 
     edge = lax.broadcasted_iota(jnp.int32, (1, SPAN), 1) + span * SPAN
     live = jnp.where(edge < count_ref[0], 1.0, 0.0)
     target = target_ref[span]
-    slots = slots_ref[span]
+    slots = slots_ref[pl.ds(span, 1)]
 
     def score_turn(t, carried):
         peak, pos = carried
         rows = pl.ds(pl.multiple_of(t * tile, tile), tile)
-        t0, t1, t2 = parts_ref[0, rows], parts_ref[1, rows], parts_ref[2, rows]
-        q0, q1, q2 = query_parts_ref[0], query_parts_ref[1], query_parts_ref[2]
-        small = mxu(t0, q2, NT) + mxu(t2, q0, NT) + mxu(t1, q1, NT)
-        score = (small + (mxu(t0, q1, NT) + mxu(t1, q0, NT))) + mxu(t0, q0, NT)
+        t0, t1 = parts_ref[0, rows], parts_ref[1, rows]
+        q0, q1 = query_parts_ref[0], query_parts_ref[1]
+        score = (mxu(t0, q1, NT) + mxu(t1, q0, NT)) + mxu(t0, q0, NT)
         score_ref[rows] = score
         number = lax.broadcasted_iota(jnp.int32, (tile, 1), 0) + t * tile
         times = jnp.sum(jnp.where(slots == number, 1.0, 0.0), axis=1, keepdims=True)
@@ -581,9 +595,9 @@
     parts, tail = load_packed(moved, owned)
     parts.append(tail)
     gradient = [dense_own[c] + parts[c] for c in range(4)]
-    entity_wide = load_wide(entity_ref, slice(None), owned, last)
+    entity_wide = load_turned(entity_ref)
     fresh = updated(entity_wide, column_of(entity_state_ref, 0, owned), gradient)
-    store_narrow(entity_new_ref, slice(None), fresh)
+    store_turned(entity_new_ref, fresh)
 
     def forward(k, carried):
         frm = lax.rem(across + k, ACROSS)
@@ -648,7 +662,7 @@
 
 def front_part(
     sizes, team,
-    entity_ref, relation_ref, source_index_ref, target_index_ref, edge_source_ref, edge_relation_ref,
+    entity_ref, relation_ref, source_index_ref, edge_source_ref, edge_relation_ref,
     table_ref, heads_ref, rels_ref, queries_ref, moved_index_ref,
     esend, evia, erecv, isend, irecv, eparts, rparts, sparts, pick, ssend, srecv, tsend, trecv, values, last,
     e_s, e_r, e_v, e_h, i_s, i_r, s_s, s_r, t_s, t_r,
@@ -661,8 +675,7 @@
     tile = 256
     stages = ((0, block), (block, block), (2 * block, packed_rows(block) - 2 * block))
 
-    isend[...] = target_index_ref[...]
-    wide = load_wide(entity_ref, slice(None), owned, last)
+    wide = load_turned(entity_ref)
     for c in range(3):
         esend[c * owned : (c + 1) * owned] = wide[c]
     esend[3 * owned :] = pack_tail(wide[3])
@@ -825,7 +838,7 @@
     count_ref, entity_ref, entity_state_ref, relation_ref, relation_state_ref,
     source_index_ref, target_index_ref, edge_source_ref, edge_relation_ref, edge_target_ref, slots_ref,
     entity_new_ref, relation_new_ref, loss_ref,
-    table, heads, rels, queries, query_grad, target_grad, moved_index,
+    table, heads, rels, queries, query_grad, target_grad, moved_index, source_index,
     esend, evia, erecv, isend, irecv, eparts, rparts, tparts, query_parts, pick, ssend, srecv, tsend, trecv,
     values, last, part, times,
     trecv_back, srecv_back, via_back, moved, own,
@@ -842,9 +855,17 @@
         return {"group": lax.div(m, chips) * ACROSS + across, "shard": 2 * lax.rem(m, chips) + core}
 
     team = (r2.shape[0], layer * chips + chip, member)
+    for r in range(shards // 2):
+        both = slice(2 * block * r, 2 * block * (r + 1))
+        source_index[:, both] = jnp.concatenate(
+            [source_index_ref[2 * r : 2 * r + 1], source_index_ref[2 * r + 1 : 2 * r + 2]], axis=1
+        )
+        isend[:, both] = jnp.concatenate(
+            [target_index_ref[2 * r : 2 * r + 1], target_index_ref[2 * r + 1 : 2 * r + 2]], axis=1
+        )
     front_part(
         sizes, team,
-        entity_ref, relation_ref, source_index_ref, target_index_ref, edge_source_ref, edge_relation_ref,
+        entity_ref, relation_ref, source_index, edge_source_ref, edge_relation_ref,
         table, heads, rels, queries, moved_index,
         esend, evia, erecv, isend, irecv, eparts, rparts, tparts, pick, ssend, srecv, tsend, trecv,
         values, last,
@@ -857,7 +878,7 @@
 
     def split_table(t, carried):
         rows = pl.ds(pl.multiple_of(t * tile, tile), tile)
-        for k, piece in enumerate(split3(table[rows])):
+        for k, piece in enumerate(split2(table[rows])):
             tparts[k, rows] = piece
         return carried
 
@@ -875,7 +896,7 @@
     back_part(
         sizes, team,
         target_grad, query_grad, heads, rels, edge_source_ref, edge_relation_ref,
-        relation_ref, relation_state_ref, moved_index, source_index_ref, entity_ref, entity_state_ref,
+        relation_ref, relation_state_ref, moved_index, source_index, entity_ref, entity_state_ref,
         entity_new_ref, relation_new_ref,
         tsend, trecv_back, ssend, srecv_back, esend, via_back, moved, pick, values, rparts, part, last, own,
         r0send, r0recv, r1, r1recv, r2, r2recv, r3, r3recv, r4, r5,
@@ -908,12 +929,12 @@
         in_specs=[pl.BlockSpec(memory_space=pltpu.SMEM)] + [in_vmem] * (len(operands) - 1),
         out_specs=[in_vmem] * 3,
         out_shape=[
-            jax.ShapeDtypeStruct((owned, width), f32),
+            jax.ShapeDtypeStruct((width, owned), f32),
             jax.ShapeDtypeStruct((padded, width), f32),
             jax.ShapeDtypeStruct((spans, 1, SPAN), f32),
         ],
         scratch_shapes=[
-            of_table, of_edges, of_edges, of_edges, of_edges, of_table, index,
+            of_table, of_edges, of_edges, of_edges, of_edges, of_table, index, index,
             flat, flat, flat, index, index,
             pltpu.VMEM((3, owned, WIDE), bf16),
             pltpu.VMEM((3, max(padded, edges), WIDE), bf16),
@@ -966,23 +987,23 @@
     relation_rows = jnp.pad(relation, ((0, padded - relations), (0, 0)))
     relation_states = jnp.pad(relation_state, (0, padded - relations), constant_values=1.0).reshape(1, padded)
     sizes = (shards, groups, block, owned, width)
-    source_index = src_send.reshape(1, table_rows)
+    source_index = src_send.reshape(peers, block)
     edge_sources, edge_relations = edge_source.reshape(1, edges), edge_relation.reshape(1, edges)
     entity_new, relation_new, loss = whole_step(
         sizes,
         edge_count,
-        entity,
+        entity.T,
         entity_state.reshape(1, owned),
         relation_rows,
         relation_states,
         source_index,
-        dst_send.reshape(1, table_rows),
+        dst_send.reshape(peers, block),
         edge_sources,
         edge_relations,
         edge_target.reshape(spans, 1, SPAN),
-        neg_slots.reshape(spans, 1, neg_slots.shape[1]),
+        neg_slots,
     )
-    return entity_new, relation_new[:relations], loss.reshape(edges)
+    return entity_new.T, relation_new[:relations], loss.reshape(edges)
 
 
 def solution(mesh):

time: 224 us -> 213 us (0.951)
  local copies, waits for them, and re-layouts: 19.3 us -> 12.5 us
  Pallas kernels: 203 us -> 199 us
    reshape x3 -> x0, local copies, waits for them, and re-layouts: 4.03 us -> none  [the longest x1 1.37 us: on_device(): source_index = src_send.reshape(1, table_rows)]
    pallas_call x1, Pallas kernels: 203 us -> 199 us  [whole_step(): pl.pallas_call(functools.partial(step_kernel, sizes), in_specs=[pl.BlockS...]
    unnamed x7 -> x6, local copies, waits for them, and re-layouts: 10.1 us -> 7.3 us
where the time goes in v6:
time: 213 us
  Pallas kernels  199 us (93%)
  local copies, waits for them, and re-layouts  12.5 us (6%)
    pallas_call x1, Pallas kernels, whole_step(): pl.pallas_call(functools.partial(step_kernel, sizes), in_specs=[pl.BlockS...  199 us
    unnamed x6, local copies, waits for them, and re-layouts  7.3 us

profile of v6, /device:TPU:69, one launch (start us, length us, event | category | flops | bytes accessed | tf_op | source)
XLA Modules:
  0.0 212.5 jit_solution(18191259229970328439)
XLA Ops:
  1.3 0.7 pad.9
  2.0 0.6 reshape.31.relation_state_ref
  2.6 2.5 %copy.14 = f32[1345,400]{1,0:T(8,128)S(1)} copy(f32[1345,400]{0,1:T(8,128)} %param.13) | data formatting | bytes 4304000 | tf_op args[2]
  5.1 1.9 pad.8.relation_ref
  6.9 198.7 %whole_step.1 = (f32[400,512]{1,0:T(8,128)}, f32[1408,400]{1,0:T(8,128)}, f32[2,1,512]{2,1,0:T(1,128)}) custom-call(s32[1]{0:T(128)S(6)} %copy.18.count_ref, f32[400,512]{1,0:T(8,128)} %bitcast.9, f32[1,512]{1,0:T(1,128)} %bitcast.17, f32[1408,400]{1,0:T(8,128)} %pad.8.relation_ref, f32[1,1408]{1,0:T(1,128)} %reshape.31.relation_state_ref, ...), custom_call_target="tpu_custom_call" | custom-call | tf_op jit(solution)/shard_map/whole_step/pallas_call | solution.py:927
  205.7 2.0 slice.3
  207.7 0.0 copy-start
  207.7 2.1 copy.15
  209.8 2.1 copy.19
  211.9 0.0 copy-done
  211.9 0.6 copy.20
Async XLA Ops:
  207.7 4.2 %copy-start = (f32[2,1,512]{2,1,0:T(1,128)S(1)}, f32[2,1,512]{2,1,0:T(1,128)}, u32[]{:S(2)}) copy-start(f32[2,1,512]{2,1,0:T(1,128)} %get-tuple-element.8) | copy-start | bytes 12292
